TPU v7x, 128 devices: a whole 4x4x4 slice. The times are simulated.
128 devices in a mesh: mem: 8 (over z_lo, y), sx: 4 (over z_hi, core), sy: 4 (over x).
Axes of the slice: x: 4, y: 4, z: 4 (z_hi: 2, z_lo: 2; z = z_hi * 2 + z_lo), core: 2. Of those that a mesh axis runs over, the one named last changes fastest.
Arguments:
- child: bfloat16 [32, 8, 192, 3072], P('mem', None, 'sx', 'sy'), may hold values from -13 to 13
Outputs:
- parent_mean: float32 [8, 64, 1024], P('mem', 'sx', 'sy')
- local_cov: float32 [64, 64, 1024], P('mem', 'sx', 'sy')
All inputs are finite; a program needn't handle non-finite values.
Results may differ from a plain program's by a relative error of at most 0.002.
Values sent between devices are 32-bit elements; how exact they have to be, the bound alone decides.
A program may use at most 192 MiB of HBM per device.

v0:
```python
import jax
import jax.numpy as jnp
import numpy as np
from jax import lax
from jax.sharding import Mesh
from jax.sharding import PartitionSpec as P

SX = ("sx_0", "sx_1")
MEM = ("mem_0", "mem_1")
MEM_SX_SY = ("mem_0", "mem_1", "sx_0", "sx_1", "sy")


def padded_2(array, sides, width):
    for axis, dim in sides:
        devices, length = (lax.axis_size(axis), array.shape[dim])
        up = [(i, (i + 1) % devices) for i in range(devices - 1)]
        down = [(j, i) for i, j in up]
        last = lax.slice_in_dim(array, length - width, length, axis=dim)
        initial = lax.slice_in_dim(array, 0, width, axis=dim)
        before = lax.ppermute(last, axis, up)
        after = lax.ppermute(initial, axis, down)
        array = jnp.concatenate([before, array, after], axis=dim)
    return array


def from_everyone(array, axis):
    copies = jnp.broadcast_to(array, (lax.axis_size(axis), *array.shape))
    return lax.all_to_all(copies, axis, split_axis=0, concat_axis=0, tiled=True)


def taken_together(array, axis):
    return from_everyone(array, axis).sum(axis=0)


def cut_along(array, dim, devices):
    shape = array.shape
    pieces = array.reshape(*shape[:dim], devices, shape[dim] // devices, *shape[dim + 1 :])
    return jnp.moveaxis(pieces, dim, 0)


def sum_at_owner(array, axis, dim):
    devices = lax.axis_size(axis)
    pieces = lax.all_to_all(cut_along(array, dim, devices), axis, 0, 0, tiled=True)
    return jnp.sum(pieces, axis=0)


def one_axis_at_a_time(array, axes):
    for axis in axes:
        array = lax.psum(array, axis)
    return array


def gaspari_table(reach):
    offsets = np.arange(-reach, reach + 1) * 1.0
    dist = np.sqrt(offsets[:, None] ** 2 + offsets[None, :] ** 2) / 2.5
    near = -0.25 * dist**5 + 0.5 * dist**4 + 0.625 * dist**3 - 5.0 / 3.0 * dist**2 + 1.0
    safe = np.maximum(dist, 0.001)
    far = (
        dist**5 / 12.0
        - 0.5 * dist**4
        + 0.625 * dist**3
        + 5.0 / 3.0 * dist**2
        - 5.0 * dist
        + 4.0
        - 2.0 / (3.0 * safe)
    )
    table = np.where(dist <= 1.0, near, np.where(dist < 2.0, far, 0.0))
    return table / table.sum()


def localize(owned, rows_dev, cols_dev):
    reach = 4
    padded = padded_2(owned, ((SX, 1), ("sy", 2)), reach)
    table = gaspari_table(reach)
    smoothed = jnp.zeros((owned.shape[0], rows_dev, cols_dev), jnp.float32)
    for first in range(2 * reach + 1):
        for second_off in range(2 * reach + 1):
            weight = float(table[first, second_off])
            if weight != 0.0:
                smoothed = (
                    smoothed
                    + weight
                    * padded[:, first : first + rows_dev, second_off : second_off + cols_dev]
                )
    return smoothed


def local(child):
    members_dev, levels, child_rows, child_cols = child.shape
    rows_dev = child_rows // 3
    cols_dev = child_cols // 3
    groups = lax.axis_size(MEM)
    members = members_dev * groups
    pairs_dev = levels * levels // groups
    level_dev = levels // groups
    device = lax.axis_index(MEM)
    parent = (
        jnp.sum(
            child.reshape(members_dev, levels, rows_dev, 3, cols_dev, 3),
            axis=(3, 5),
            dtype=jnp.float32,
        )
        / 9.0
    )
    totals = taken_together(jnp.sum(parent, axis=0), MEM)
    first_pair = device * pairs_dev
    pair_ids = first_pair + jnp.arange(pairs_dev, dtype=jnp.int32)
    diag_mask = (pair_ids // levels == pair_ids % levels).astype(jnp.float32)
    own_left = pair_ids // levels
    own_right = pair_ids % levels
    products = jnp.einsum("alxy,akxy->lkxy", parent, parent).reshape(
        levels * levels, rows_dev, cols_dev
    )
    second = sum_at_owner(products, MEM, 0)
    parent_mean = totals / members
    outer_own = jnp.take(parent_mean, own_left, axis=0) * jnp.take(parent_mean, own_right, axis=0)
    owned = (second - members * outer_own) / (members - 1)
    variance_total = one_axis_at_a_time(jnp.sum(owned * diag_mask[:, None, None]), MEM_SX_SY)
    cells = levels * rows_dev * lax.axis_size(SX) * cols_dev * lax.axis_size("sy")
    spread = variance_total / cells
    smoothed = localize(owned, rows_dev, cols_dev)
    local_cov = smoothed / (spread + 1e-06)
    mean_rows = lax.dynamic_slice_in_dim(parent_mean, device * level_dev, level_dev, 0)
    return (mean_rows, local_cov)


def solution(mesh):
    split = Mesh(
        mesh.devices.reshape(2, 4, 2, 2, mesh.shape["sy"]), ("mem_0", "mem_1", "sx_0", "sx_1", "sy")
    )
    in_specs = (P(MEM, None, SX, "sy"),)
    out_specs = (P(MEM, SX, "sy"), P(MEM, SX, "sy"))
    return jax.shard_map(local, mesh=split, in_specs=in_specs, out_specs=out_specs, check_vma=False)
```

profile of v0, /device:TPU:1, one launch (start us, length us, event | category | flops | bytes accessed | tf_op | source)
XLA Modules:
  0.0 192.7 jit_solution(8991469457047343743)
XLA Ops:
  0.6 37.3 %copy.9 = f32[4,8,48,768]{1,0,3,2:T(4,128)} copy(bf16[4,8,48,768]{3,2,1,0:T(8,128)(2,1)} %param.3) | data formatting | bytes 7077888 | tf_op jit(solution)/shard_map/convert_element_type | solution.py:98
  37.9 42.6 %reduce_sum.45 = f32[4,8,16,256]{1,0,3,2:T(4,128)} reduce(f32[4,8,16,3,256,3]{1,0,5,4,3,2:T(4,128)} %bitcast, f32[]{:T(128)} %constant.74.clone.1), dimensions={3,5}, to_apply=%region_0.0 | reduce | flops 1048576 | bytes 5242884 | tf_op jit(solution)/shard_map/reduce_sum | solution.py:98
  80.5 10.0 %multiply_reduce_fusion = f32[8,16,256]{0,2,1:T(8,128)S(1)} fusion(f32[4,8,16,256]{1,0,3,2:T(4,128)} %reduce_sum.45), kind=kLoop, calls=%fused_computation.4 | loop fusion | flops 229376 | bytes 655360 | tf_op jit(solution)/shard_map/reduce_sum | solution.py:105
  90.6 0.6 copy.10
  91.1 1.1 broadcast_in_dim.13
  92.3 6.4 %all-to-all-start = ((f32[8,8,16,256]{3,2,1,0:T(8,128)}), f32[8,8,16,256]{3,2,1,0:T(8,128)S(1)}, u32[]{:S(2)}, u32[]{:S(2)}) async-start(f32[8,8,16,256]{3,2,1,0:T(8,128)} %broadcast_in_dim.13), calls=%async_computation | async-start | bytes 2097152 | tf_op jit(solution)/shard_map/all_to_all | solution.py:28
  98.6 14.8 %convolution_bitcast_fusion = f32[8,8,16,256]{0,1,3,2:T(8,128)} fusion(f32[4,8,16,256]{1,0,3,2:T(4,128)} %reduce_sum.45), kind=kOutput, calls=%fused_computation.2 | convolution fusion | flops 2228224 | bytes 1572864 | tf_op jit(solution)/shard_map/alxy,akxy->lkxy/dot_general | solution.py:111
  113.4 9.1 %copy.11 = f32[8,8,16,256]{3,2,1,0:T(8,128)} copy(f32[8,8,16,256]{0,1,3,2:T(8,128)} %convolution_bitcast_fusion) | data formatting | bytes 2097152 | tf_op jit(solution)/shard_map/alxy,akxy->lkxy/transpose | solution.py:111
  122.6 0.0 all-to-all-done
  122.6 5.1 %all-to-all-start.1 = ((f32[8,8,16,256]{3,2,1,0:T(8,128)}), f32[8,8,16,256]{3,2,1,0:T(8,128)S(1)}, u32[]{:S(2)}, u32[]{:S(2)}) async-start(f32[8,8,16,256]{3,2,1,0:T(8,128)} %copy.11), calls=%async_computation.1 | async-start | bytes 2097152 | tf_op jit(solution)/shard_map/all_to_all | solution.py:43
  127.8 0.1 reduce_sum.47
  127.9 0.6 gather_fusion.1
  128.5 0.6 gather_fusion
  129.0 14.6 %all-to-all-done.1 = f32[8,8,16,256]{3,2,1,0:T(8,128)S(1)} async-done(((f32[8,8,16,256]{3,2,1,0:T(8,128)}), f32[8,8,16,256]{3,2,1,0:T(8,128)S(1)}, u32[]{:S(2)}, u32[]{:S(2)}) %all-to-all-start.1) | async-done | bytes 1048608 | tf_op jit(solution)/shard_map/all_to_all | solution.py:43
  143.6 0.1 reduce_sum.48
  143.7 0.7 multiply_reduce_fusion.1
  144.4 2.7 %collective-permute-start.1 = (f32[8,4,256]{2,1,0:T(4,128)S(1)}, f32[8,4,256]{2,1,0:T(4,128)S(1)}, u32[]{:S(2)}, u32[]{:S(2)}) collective-permute-start(f32[8,4,256]{2,1,0:T(4,128)S(1)} %get-tuple-element.10), channel_id=1, source_target_pairs={{4,0},{8,4},{12,8},{5,1},{9,5},{13,9},{6,2},{10,6},{14,10},{7,3},{... | collective-permute-start | bytes 98312 | tf_op jit(solution)/shard_map/ppermute | solution.py:21
  147.1 5.1 %collective-permute-start = (f32[8,4,256]{2,1,0:T(4,128)S(1)}, f32[8,4,256]{2,1,0:T(4,128)S(1)}, u32[]{:S(2)}, u32[]{:S(2)}) collective-permute-start(f32[8,4,256]{2,1,0:T(4,128)S(1)} %get-tuple-element.9), channel_id=1, source_target_pairs={{0,4},{4,8},{8,12},{1,5},{5,9},{9,13},{2,6},{6,10},{10,14},{3,7},{... | collective-permute-start | bytes 98312 | tf_op jit(solution)/shard_map/ppermute | solution.py:20
  152.3 4.4 %psum.35 = f32[]{:T(128)} all-reduce(f32[]{:T(128)} %get-tuple-element.3), channel_id=1, replica_groups=mesh['mem_0'=2,'mem_1'=4,'sx_0'=2,'sx_1'=2,'sy'=4] {'mem_0'}, use_global_device_ids=true, to_apply=%region_5.7 | all-reduce | flops 1 | bytes 8 | tf_op jit(solution)/shard_map/psum | solution.py:49
  156.7 7.3 %psum.36 = f32[]{:T(128)} all-reduce(f32[]{:T(128)} %psum.35), channel_id=1, replica_groups=mesh['mem_0'=2,'mem_1'=4,'sx_0'=2,'sx_1'=2,'sy'=4] {'mem_1'}, use_global_device_ids=true, to_apply=%region_6.8 | all-reduce | flops 1 | bytes 8 | tf_op jit(solution)/shard_map/psum | solution.py:49
  163.9 5.9 %psum.37 = f32[]{:T(128)} all-reduce(f32[]{:T(128)} %psum.36), channel_id=1, replica_groups=mesh['mem_0'=2,'mem_1'=4,'sx_0'=2,'sx_1'=2,'sy'=4] {'sx_0'}, use_global_device_ids=true, to_apply=%region_7.9 | all-reduce | flops 1 | bytes 8 | tf_op jit(solution)/shard_map/psum | solution.py:49
  169.8 4.3 %psum.38 = f32[]{:T(128)} all-reduce(f32[]{:T(128)} %psum.37), channel_id=1, replica_groups=mesh['mem_0'=2,'mem_1'=4,'sx_0'=2,'sx_1'=2,'sy'=4] {'sx_1'}, use_global_device_ids=true, to_apply=%region_8.10 | all-reduce | flops 1 | bytes 8 | tf_op jit(solution)/shard_map/psum | solution.py:49
  174.2 0.0 collective-permute-done.1
  174.2 0.0 collective-permute-done
  174.2 0.1 fusion.89
  174.3 3.1 %collective-permute-start.2 = (f32[8,24,4]{2,1,0:T(8,128)S(1)}, f32[8,24,4]{2,1,0:T(8,128)S(1)}, u32[]{:S(2)}, u32[]{:S(2)}) collective-permute-start(f32[8,24,4]{2,1,0:T(8,128)S(1)} %get-tuple-element.7), channel_id=1, source_target_pairs={{0,1},{1,2},{2,3},{4,5},{5,6},{6,7},{8,9},{9,10},{10,11},{12,13},{... | collective-permute-start | bytes 9224 | tf_op jit(solution)/shard_map/ppermute | solution.py:20
  177.4 1.3 collective-permute-start.3
  178.7 0.6 constant_dynamic-slice_fusion
  179.3 9.9 %psum.39 = f32[]{:T(128)} all-reduce(f32[]{:T(128)} %psum.38), channel_id=1, replica_groups=mesh['mem_0'=2,'mem_1'=4,'sx_0'=2,'sx_1'=2,'sy'=4] {'sy'}, use_global_device_ids=true, to_apply=%region_9.11 | all-reduce | flops 1 | bytes 8 | tf_op jit(solution)/shard_map/psum | solution.py:49
  189.9 0.0 collective-permute-done.2
  189.9 0.0 collective-permute-done.3
  190.0 0.2 maximum_maximum_fusion
  190.2 2.6 %fusion.13 = f32[8,16,256]{2,1,0:T(8,128)} fusion(f32[8,16,256]{2,1,0:T(8,128)S(1)} %broadcast_multiply_fusion, f32[8,4,256]{2,1,0:T(4,128)S(1)} %collective-permute-done.1, f32[8,24,260]{2,1,0:T(8,128)S(1)} %get-tuple-element.6, f32[8,24,260]{2,1,0:T(8,128)S(1)} %get-tuple-element.5, f32[8,4,256]{2,1,0:T(4,128)S(1)} %collective-permute-done, ...), kind=kLoop, calls=%fused_computation.32 | loop fusion | flops 4784128 | bytes 8323076 | tf_op jit(solution)/shard_map/div | solution.py:122
  (9 shorter events, 0.1 us)
Async XLA Ops:
  92.3 30.3 %all-to-all-start = ((f32[8,8,16,256]{3,2,1,0:T(8,128)}), f32[8,8,16,256]{3,2,1,0:T(8,128)S(1)}, u32[]{:S(2)}, u32[]{:S(2)}) async-start(f32[8,8,16,256]{3,2,1,0:T(8,128)} %broadcast_in_dim.13), calls=%async_computation | async-start | bytes 2097152 | tf_op jit(solution)/shard_map/all_to_all | solution.py:28
  122.6 21.0 %all-to-all-start.1 = ((f32[8,8,16,256]{3,2,1,0:T(8,128)}), f32[8,8,16,256]{3,2,1,0:T(8,128)S(1)}, u32[]{:S(2)}, u32[]{:S(2)}) async-start(f32[8,8,16,256]{3,2,1,0:T(8,128)} %copy.11), calls=%async_computation.1 | async-start | bytes 2097152 | tf_op jit(solution)/shard_map/all_to_all | solution.py:43
  144.4 29.7 %collective-permute-start.1 = (f32[8,4,256]{2,1,0:T(4,128)S(1)}, f32[8,4,256]{2,1,0:T(4,128)S(1)}, u32[]{:S(2)}, u32[]{:S(2)}) collective-permute-start(f32[8,4,256]{2,1,0:T(4,128)S(1)} %get-tuple-element.10), channel_id=1, source_target_pairs={{4,0},{8,4},{12,8},{5,1},{9,5},{13,9},{6,2},{10,6},{14,10},{7,3},{... | collective-permute-start | bytes 98312 | tf_op jit(solution)/shard_map/ppermute | solution.py:21
  147.1 27.0 %collective-permute-start = (f32[8,4,256]{2,1,0:T(4,128)S(1)}, f32[8,4,256]{2,1,0:T(4,128)S(1)}, u32[]{:S(2)}, u32[]{:S(2)}) collective-permute-start(f32[8,4,256]{2,1,0:T(4,128)S(1)} %get-tuple-element.9), channel_id=1, source_target_pairs={{0,4},{4,8},{8,12},{1,5},{5,9},{9,13},{2,6},{6,10},{10,14},{3,7},{... | collective-permute-start | bytes 98312 | tf_op jit(solution)/shard_map/ppermute | solution.py:20
  174.3 15.6 %collective-permute-start.2 = (f32[8,24,4]{2,1,0:T(8,128)S(1)}, f32[8,24,4]{2,1,0:T(8,128)S(1)}, u32[]{:S(2)}, u32[]{:S(2)}) collective-permute-start(f32[8,24,4]{2,1,0:T(8,128)S(1)} %get-tuple-element.7), channel_id=1, source_target_pairs={{0,1},{1,2},{2,3},{4,5},{5,6},{6,7},{8,9},{9,10},{10,11},{12,13},{... | collective-permute-start | bytes 9224 | tf_op jit(solution)/shard_map/ppermute | solution.py:20
  177.4 12.5 %collective-permute-start.3 = (f32[8,24,4]{2,1,0:T(8,128)S(1)}, f32[8,24,4]{2,1,0:T(8,128)S(1)}, u32[]{:S(2)}, u32[]{:S(2)}) collective-permute-start(f32[8,24,4]{2,1,0:T(8,128)S(1)} %get-tuple-element.8), channel_id=1, source_target_pairs={{1,0},{2,1},{3,2},{5,4},{6,5},{7,6},{9,8},{10,9},{11,10},{13,12},{... | collective-permute-start | bytes 9224 | tf_op jit(solution)/shard_map/ppermute | solution.py:21
where the time goes:
time: 196 us; the launch traced here: 193 us
  other arithmetic  56.4 us (29%)
  local copies, waits for them, and re-layouts  50 us (26%)
  blocking collectives  31.8 us (16%)
  starting transfers between devices  23.7 us (12%)
  matrix products  14.8 us (8%)
  waiting for transfers between devices  14.6 us (7%)
    reduce_sum x1, other arithmetic, local(): jnp.sum(child.reshape(members_dev, levels, rows_dev, 3, cols_dev, 3), axi...  42.6 us
    convert_element_type x1, local copies, waits for them, and re-layouts, local(): jnp.sum(child.reshape(members_dev, levels, rows_dev, 3, cols_dev, 3), axi...  37.3 us
    psum x5, blocking collectives, one_axis_at_a_time(): array = lax.psum(array, axis)  31.8 us
    dot_general x1, matrix products, local(): jnp.einsum('alxy,akxy->lkxy', parent, parent)  14.8 us
    all_to_all x1, waiting for transfers between devices, sum_at_owner(): lax.all_to_all(cut_along(array, dim, devices), axis, 0, 0, tiled=True)  14.6 us
    reduce_sum x1, other arithmetic, local(): totals = taken_together(jnp.sum(parent, axis=0), MEM)  10 us
    transpose x1, local copies, waits for them, and re-layouts, local(): jnp.einsum('alxy,akxy->lkxy', parent, parent)  9.14 us
    ppermute x2, starting transfers between devices, padded_2(): before = lax.ppermute(last, axis, up)  8.23 us
  transfers between devices with their start and end apart: 6, of which 1 were waited for; matrix products, arithmetic and copies ran while one was open for 13% of the time, Pallas kernels for 0%

commit v1 on v0

v1 whole, which is shorter than its diff:
```python
import functools

import jax
import jax.numpy as jnp
import numpy as np
from jax import lax
from jax.experimental import pallas as pl
from jax.experimental.pallas import tpu as pltpu
from jax.sharding import PartitionSpec as P

MESH = pl.DeviceIdType.MESH
REACH = 4
LANES = 128
SUB = 8


def gaspari_table(reach):
    offsets = np.arange(-reach, reach + 1) * 1.0
    dist = np.sqrt(offsets[:, None] ** 2 + offsets[None, :] ** 2) / 2.5
    near = -0.25 * dist**5 + 0.5 * dist**4 + 0.625 * dist**3 - 5.0 / 3.0 * dist**2 + 1.0
    safe = np.maximum(dist, 0.001)
    far = (
        dist**5 / 12.0
        - 0.5 * dist**4
        + 0.625 * dist**3
        + 5.0 / 3.0 * dist**2
        - 5.0 * dist
        + 4.0
        - 2.0 / (3.0 * safe)
    )
    table = np.where(dist <= 1.0, near, np.where(dist < 2.0, far, 0.0))
    return table / table.sum()


def kernel(
    nmem,
    nsx,
    nsy,
    child_ref,
    mean_ref,
    cov_ref,
    xbuf,
    ybuf,
    psend,
    rbuf,
    abuf,
    mbuf,
    msg,
    q,
    edge_l,
    edge_r,
    hsend,
    h,
    zbuf,
    s1,
    s2,
    ld_sem,
    p1_send,
    p1_recv,
    s1_send,
    s1_recv,
    e_send,
    e_recv,
    q_send,
    q_recv,
    r_send,
    h_send,
    h_recv,
    g_send,
    s2_send,
    s2_recv,
):
    members, levels, child_rows, child_cols = child_ref.shape
    rows = child_rows // 3
    mem = lax.axis_index("mem")
    sx = lax.axis_index("sx")
    sy = lax.axis_index("sy")
    total_members = members * nmem

    def at(m, x, y):
        return {"mem": m, "sx": x, "sy": y}

    loads = []
    for m in range(members):
        copy = pltpu.make_async_copy(child_ref.at[m], xbuf.at[m], ld_sem.at[m])
        copy.start()
        loads.append(copy)

    barrier = pltpu.get_barrier_semaphore()
    greeted = 0

    def greet(m, x, y):
        pl.semaphore_signal(barrier, inc=1, device_id=at(m, x, y), device_id_type=MESH)

    mem_peers = [lax.rem(mem + o, nmem) for o in range(nmem)]
    plane = [(a, b) for a in range(nsx) for b in range(nsy) if (a, b) != (0, 0)]
    plane_peers = [(lax.rem(sx + a, nsx), lax.rem(sy + b, nsy)) for a, b in plane]
    for o in range(1, nmem):
        greet(mem_peers[o], sx, sy)
        greeted += 1
    for x, y in plane_peers:
        greet(mem, x, y)
        greeted += 1
    for a in (1, nsx - 1):
        for o in range(1, nmem):
            greet(mem_peers[o], lax.rem(sx + a, nsx), sy)
            greeted += 1

    zero = jnp.zeros((SUB, LANES), jnp.float32)

    @pl.when(sx == 0)
    def _():
        for s in range(2):
            for v in range(5):
                q[s, v] = zero
            for v in range(2):
                h[s, v] = zero

    @pl.when(sx == nsx - 1)
    def _():
        for s in range(nmem + 2, nmem + 4):
            for v in range(5):
                q[s, v] = zero
            for v in range(2):
                h[s, v] = zero

    @pl.when(sy == 0)
    def _():
        for l in range(levels):
            for i in range(2):
                edge_l[l, i] = zero

    @pl.when(sy == nsy - 1)
    def _():
        for l in range(levels):
            for i in range(2):
                edge_r[l, i] = zero

    r_ids = lax.broadcasted_iota(jnp.int32, (child_cols, child_cols // 3), 0)
    c_ids = lax.broadcasted_iota(jnp.int32, (child_cols, child_cols // 3), 1)
    off = r_ids - 3 * c_ids
    pick = jnp.where((off >= 0) & (off <= 2), 1.0, 0.0).astype(jnp.bfloat16)

    p1 = []
    for m in range(members):
        loads[m].wait()
        y = jnp.dot(
            xbuf[m].reshape(levels * child_rows, child_cols),
            pick,
            preferred_element_type=jnp.float32,
        )
        for c in range(2):
            ybuf[m % 2, c] = y[:, c * LANES : (c + 1) * LANES]
        for i in range(rows):
            for c in range(2):
                total = ybuf[m % 2, c, pl.ds(3 * i, levels, stride=child_rows), :]
                for a in (1, 2):
                    total += ybuf[m % 2, c, pl.ds(3 * i + a, levels, stride=child_rows), :]
                psend[i // 2, m, 2 * c + i % 2] = total
        if m == 0:
            pl.semaphore_wait(barrier, greeted)
        for o in range(1, nmem):
            copy = pltpu.make_async_remote_copy(
                src_ref=psend.at[mem_peers[o], m],
                dst_ref=rbuf.at[o, m],
                send_sem=p1_send.at[o, m],
                recv_sem=p1_recv.at[o, m],
                device_id=at(mem_peers[o], sx, sy),
                device_id_type=MESH,
            )
            copy.start()
            p1.append(copy)
        for v in range(4):
            rbuf[0, m, v] = psend[mem, m, v]
    for copy in p1:
        copy.wait_recv()

    def anomalies(v, var):
        total = zero
        for o in range(nmem):
            for m in range(members):
                total += rbuf[o, m, v]
        mean = total * (1.0 / total_members)
        mbuf[v] = mean * (1.0 / 9.0)
        for o in range(nmem):
            for m in range(members):
                anom = rbuf[o, m, v] - mean
                abuf[v, o * members + m] = anom
                var += anom * anom
        return var

    var = lax.fori_loop(0, 4, anomalies, zero)
    s1[0] = var
    s1_copies = []
    for o in range(1, nmem):
        copy = pltpu.make_async_remote_copy(
            src_ref=s1.at[0],
            dst_ref=s1.at[o],
            send_sem=s1_send.at[o],
            recv_sem=s1_recv.at[o],
            device_id=at(mem_peers[o], sx, sy),
            device_id_type=MESH,
        )
        copy.start()
        s1_copies.append(copy)

    factor = 1.0 / (81.0 * (total_members - 1))

    def covariances(v, carry):
        acc = [zero] * levels
        for t in range(total_members):
            anom = abuf[v, t]
            for l in range(levels):
                acc[l] += anom * abuf[v, t, pl.ds(l, 1), :]
        for l in range(levels):
            msg[l, v] = acc[l] * factor
        return carry

    lax.fori_loop(0, 4, covariances, 0)
    for l in range(levels):
        msg[l, 4] = zero
        for v in range(4):
            msg[l, 4, pl.ds(v, 1), :] = mbuf[v, pl.ds(l, 1), :]

    def to_right():
        return pltpu.make_async_remote_copy(
            src_ref=msg.at[:, pl.ds(2, 2)],
            dst_ref=edge_l,
            send_sem=e_send.at[0],
            recv_sem=e_recv.at[0],
            device_id=at(mem, sx, lax.rem(sy + 1, nsy)),
            device_id_type=MESH,
        )

    def to_left():
        return pltpu.make_async_remote_copy(
            src_ref=msg.at[:, pl.ds(0, 2)],
            dst_ref=edge_r,
            send_sem=e_send.at[1],
            recv_sem=e_recv.at[1],
            device_id=at(mem, sx, lax.rem(sy + nsy - 1, nsy)),
            device_id_type=MESH,
        )

    @pl.when(sy < nsy - 1)
    def _():
        to_right().start()

    @pl.when(sy > 0)
    def _():
        to_left().start()

    def to_owner(src, dst, slot, owner, x, send, recv):
        return pltpu.make_async_remote_copy(
            src_ref=src.at[owner],
            dst_ref=dst.at[slot],
            send_sem=send,
            recv_sem=recv.at[slot],
            device_id=at(owner, x, sy),
            device_id_type=MESH,
        )

    def to_tile(src, dst, send, recv):
        return [
            to_owner(src, dst, mem + 2, mem_peers[o], sx, send.at[o], recv)
            for o in range(1, nmem)
        ]

    def to_low(src, dst, send, recv):
        low = lax.rem(sx + nsx - 1, nsx)
        slot = mem + nmem + 2
        return [to_owner(src, dst, slot, l, low, send.at[l], recv) for l in range(nmem)]

    def to_high(src, dst, send, recv):
        high = lax.rem(sx + 1, nsx)
        slot = mem - (nmem - 2)
        return [to_owner(src, dst, slot, l, high, send.at[l], recv) for l in range(nmem)]

    sends_down = (mem < 2) & (sx > 0)
    sends_up = (mem >= nmem - 2) & (sx < nsx - 1)

    def start_all(src, dst, send_tile, send_next, recv):
        for copy in to_tile(src, dst, send_tile, recv):
            copy.start()
        @pl.when(sends_down)
        def _():
            for copy in to_low(src, dst, send_next, recv):
                copy.start()
        @pl.when(sends_up)
        def _():
            for copy in to_high(src, dst, send_next, recv):
                copy.start()

    start_all(msg, q, q_send, r_send, q_recv)
    for v in range(5):
        q[mem + 2, v] = msg[mem, v]

    @pl.when(sy < nsy - 1)
    def _():
        to_left().wait_recv()

    @pl.when(sy > 0)
    def _():
        to_right().wait_recv()

    lane = lax.broadcasted_iota(jnp.int32, (SUB, LANES), 1)
    low_half = lane < LANES // 2
    for l in range(levels):
        for i in range(2):
            hsend[l, i] = jnp.where(low_half, edge_r[l, i], edge_l[l, i])
    start_all(hsend, h, h_send, g_send, h_recv)
    for v in range(2):
        h[mem + 2, v] = hsend[mem, v]

    for copy in s1_copies:
        copy.wait_recv()
    tile = s1[0]
    for o in range(1, nmem):
        tile += s1[o]
    s2[0] = tile
    s2_copies = []
    for n, (x, y) in enumerate(plane_peers):
        copy = pltpu.make_async_remote_copy(
            src_ref=s2.at[0],
            dst_ref=s2.at[n + 1],
            send_sem=s2_send.at[n + 1],
            recv_sem=s2_recv.at[n + 1],
            device_id=at(mem, x, y),
            device_id_type=MESH,
        )
        copy.start()
        s2_copies.append(copy)

    def arrived(dst, recv, slot):
        pltpu.make_async_remote_copy(
            src_ref=dst.at[slot],
            dst_ref=dst.at[slot],
            send_sem=q_send.at[0],
            recv_sem=recv.at[slot],
            device_id=at(mem_peers[1], sx, sy),
            device_id_type=MESH,
        ).wait_recv()

    for dst, recv in ((q, q_recv), (h, h_recv)):
        for o in range(1, nmem):
            arrived(dst, recv, mem_peers[o] + 2)

        @pl.when(sx > 0)
        def _():
            for slot in range(2):
                arrived(dst, recv, slot)

        @pl.when(sx < nsx - 1)
        def _():
            for slot in range(nmem + 2, nmem + 4):
                arrived(dst, recv, slot)

    for d in range(nmem):
        for i in range(2):
            for c in range(2):
                mean_ref[0, pl.ds(2 * d + i, 1), pl.ds(c * LANES, LANES)] = q[
                    d + 2, 4, pl.ds(2 * c + i, 1), :
                ]

    table = gaspari_table(REACH)

    def cells(i):
        slot, i2 = i // 2, i % 2
        return jnp.concatenate([q[slot, i2], q[slot, 2 + i2], h[slot, i2]], axis=1)

    for i in range(rows):
        center = i + REACH
        lines = [cells(center)]
        for e in range(1, REACH + 1):
            lines.append(cells(center - e) + cells(center + e))
        out = None
        for f in range(REACH + 1):
            line = None
            for e in range(REACH + 1):
                weight = float(table[REACH + e, REACH + f])
                if weight != 0.0:
                    term = weight * lines[e]
                    line = term if line is None else line + term
            if f == 0:
                out = line
            else:
                width = 3 * LANES
                out = out + pltpu.roll(line, f, 1) + pltpu.roll(line, width - f, 1)
        for c in range(2):
            zbuf[c, pl.ds(i, levels, stride=rows), :] = out[:, c * LANES : (c + 1) * LANES]

    for copy in s2_copies:
        copy.wait_recv()
    everyone = s2[0]
    for n in range(len(s2_copies)):
        everyone += s2[n + 1]
    count = levels * rows * nsx * child_cols // 3 * nsy
    spread = jnp.sum(everyone, keepdims=True) * (factor / count)
    scale = 1.0 / (spread + 1e-6)
    for k in range(levels):
        for c in range(2):
            cov_ref[k, :, pl.ds(c * LANES, LANES)] = zbuf[c, pl.ds(k * rows, rows), :] * scale

    for copy in p1 + s1_copies + s2_copies:
        copy.wait_send()
    for src, dst, tile_sem, next_sem, recv in (
        (msg, q, q_send, r_send, q_recv),
        (hsend, h, h_send, g_send, h_recv),
    ):
        for copy in to_tile(src, dst, tile_sem, recv):
            copy.wait_send()

        @pl.when(sends_down)
        def _():
            for copy in to_low(src, dst, next_sem, recv):
                copy.wait_send()

        @pl.when(sends_up)
        def _():
            for copy in to_high(src, dst, next_sem, recv):
                copy.wait_send()

    @pl.when(sy < nsy - 1)
    def _():
        to_right().wait_send()

    @pl.when(sy > 0)
    def _():
        to_left().wait_send()


def solution(mesh):
    nmem, nsx, nsy = (mesh.shape[name] for name in ("mem", "sx", "sy"))

    def local(child):
        members, levels, child_rows, child_cols = child.shape
        rows, cols = child_rows // 3, child_cols // 3
        f32 = jnp.float32
        dma = pltpu.SemaphoreType.DMA
        return pl.pallas_call(
            functools.partial(kernel, nmem, nsx, nsy),
            out_shape=(
                jax.ShapeDtypeStruct((levels // nmem, rows, cols), f32),
                jax.ShapeDtypeStruct((levels, rows, cols), f32),
            ),
            in_specs=[pl.BlockSpec(memory_space=pl.ANY)],
            out_specs=(
                pl.BlockSpec(memory_space=pltpu.VMEM),
                pl.BlockSpec(memory_space=pltpu.VMEM),
            ),
            scratch_shapes=[
                pltpu.VMEM(child.shape, child.dtype),
                pltpu.VMEM((2, 2, levels * child_rows, LANES), f32),
                pltpu.VMEM((nmem, members, 4, SUB, LANES), f32),
                pltpu.VMEM((nmem, members, 4, SUB, LANES), f32),
                pltpu.VMEM((4, nmem * members, SUB, LANES), f32),
                pltpu.VMEM((4, SUB, LANES), f32),
                pltpu.VMEM((levels, 5, SUB, LANES), f32),
                pltpu.VMEM((nmem + 4, 5, SUB, LANES), f32),
                pltpu.VMEM((levels, 2, SUB, LANES), f32),
                pltpu.VMEM((levels, 2, SUB, LANES), f32),
                pltpu.VMEM((levels, 2, SUB, LANES), f32),
                pltpu.VMEM((nmem + 4, 2, SUB, LANES), f32),
                pltpu.VMEM((2, levels * rows, LANES), f32),
                pltpu.VMEM((nmem, SUB, LANES), f32),
                pltpu.VMEM((nsx * nsy, SUB, LANES), f32),
                dma((members,)),
                dma((nmem, members)),
                dma((nmem, members)),
                dma((nmem,)),
                dma((nmem,)),
                dma((2,)),
                dma((2,)),
                dma((nmem,)),
                dma((nmem + 4,)),
                dma((nmem,)),
                dma((nmem,)),
                dma((nmem + 4,)),
                dma((nmem,)),
                dma((nsx * nsy,)),
                dma((nsx * nsy,)),
            ],
            compiler_params=pltpu.CompilerParams(collective_id=0, has_side_effects=True),
        )(child)

    return jax.shard_map(
        local,
        mesh=mesh,
        in_specs=(P("mem", None, "sx", "sy"),),
        out_specs=(P("mem", "sx", "sy"), P("mem", "sx", "sy")),
        check_vma=False,
    )
```

time: 196 us -> 33 us (0.17); the launches traced: 193 us -> 32.8 us
  other arithmetic: 56.4 us -> 0 us
  local copies, waits for them, and re-layouts: 50 us -> 2.89 us
  blocking collectives: 31.8 us -> 0 us
  Pallas kernels: 0 us -> 29.3 us
  starting transfers between devices: 23.7 us -> 0 us
  matrix products: 14.8 us -> 0 us
  waiting for transfers between devices: 14.6 us -> 0 us
    reduce_sum x5 -> x0, other arithmetic: 53.5 us -> none  [the longest x1 42.6 us: local(): jnp.sum(child.reshape(members_dev, levels, rows_dev, 3, cols_dev, 3), axi...]
    convert_element_type x1 -> x0, local copies, waits for them, and re-layouts: 37.3 us -> none  [local(): jnp.sum(child.reshape(members_dev, levels, rows_dev, 3, cols_dev, 3), axi...]
    psum x5 -> x0, blocking collectives: 31.8 us -> none  [one_axis_at_a_time(): array = lax.psum(array, axis)]
    pallas_call x0 -> x1, Pallas kernels: none -> 29.3 us  [local(): pl.pallas_call(functools.partial(kernel, nmem, nsx, nsy), out_shape=(jax....]
    dot_general x1 -> x0, matrix products: 14.8 us -> none  [local(): jnp.einsum('alxy,akxy->lkxy', parent, parent)]
    all_to_all x2 -> x0, waiting for transfers between devices: 14.6 us -> none  [the longest x1 14.6 us: sum_at_owner(): lax.all_to_all(cut_along(array, dim, devices), axis, 0, 0, tiled=True)]
    ppermute x4 -> x0, starting transfers between devices: 12.2 us -> none  [the longest x2 8.23 us: padded_2(): before = lax.ppermute(last, axis, up)]
    all_to_all x2 -> x0, starting transfers between devices: 11.5 us -> none  [the longest x1 6.36 us: from_everyone(): return lax.all_to_all(copies, axis, split_axis=0, concat_axis=0, tiled=True)]
  transfers between devices with their start and end apart: 6 -> 0, of which waited for: 1 -> 0; matrix products, arithmetic and copies ran while one was open for 13% -> 0% of each run, Pallas kernels for 0% -> 0%
where the time goes in v1:
time: 33 us; the launch traced here: 32.8 us
  Pallas kernels  29.3 us (89%)
  local copies, waits for them, and re-layouts  2.89 us (9%)
  between operations  0.64 us (2%)
    pallas_call x1, Pallas kernels, local(): pl.pallas_call(functools.partial(kernel, nmem, nsx, nsy), out_shape=(jax....  29.3 us
    unnamed x2, local copies, waits for them, and re-layouts  2.89 us

profile of v1, /device:TPU:1, one launch (start us, length us, event | category | flops | bytes accessed | tf_op | source)
XLA Modules:
  0.0 32.8 jit_solution(8623242649330064465)
XLA Ops:
  0.6 29.3 %shard_map.30 = (f32[1,16,256]{2,1,0:T(8,128)}, f32[8,16,256]{2,1,0:T(8,128)}) custom-call(bf16[4,8,48,768]{3,2,1,0:T(8,128)(2,1)} %child_ref.1), custom_call_target="tpu_custom_call" | custom-call | tf_op jit(solution)/shard_map/pallas_call | solution.py:440
  30.0 1.3 %copy.5 = f32[1,16,256]{2,1,0:T(8,128)} copy(f32[1,16,256]{2,1,0:T(8,128)} %get-tuple-element.4) | data formatting | bytes 32768
  31.3 1.6 %copy.6 = f32[8,16,256]{2,1,0:T(8,128)} copy(f32[8,16,256]{2,1,0:T(8,128)} %get-tuple-element.5) | data formatting | bytes 262144

commit v2 on v0

v2 whole, which is shorter than its diff:
```python
import functools

import jax
import jax.numpy as jnp
import numpy as np
from jax import lax
from jax.experimental import pallas as pl
from jax.experimental.pallas import tpu as pltpu
from jax.sharding import PartitionSpec as P

MESH = pl.DeviceIdType.MESH
REACH = 4
LANES = 128
SUB = 8
VMEM_GRANT = 55_500_000


def gaspari_table(reach):
    offsets = np.arange(-reach, reach + 1) * 1.0
    dist = np.sqrt(offsets[:, None] ** 2 + offsets[None, :] ** 2) / 2.5
    near = -0.25 * dist**5 + 0.5 * dist**4 + 0.625 * dist**3 - 5.0 / 3.0 * dist**2 + 1.0
    safe = np.maximum(dist, 0.001)
    far = (
        dist**5 / 12.0
        - 0.5 * dist**4
        + 0.625 * dist**3
        + 5.0 / 3.0 * dist**2
        - 5.0 * dist
        + 4.0
        - 2.0 / (3.0 * safe)
    )
    table = np.where(dist <= 1.0, near, np.where(dist < 2.0, far, 0.0))
    return table / table.sum()


def gather(
    nmem,
    nsx,
    nsy,
    child_ref,
    z_ref,
    all_ref,
    means_ref,
    xbuf,
    ybuf,
    psend,
    rbuf,
    pack,
    from_left,
    from_right,
    hsend,
    hbuf,
    abuf,
    mbuf,
    mmsg,
    means,
    msg,
    q,
    odd,
    s1,
    s2,
    ld_sem,
    p1_sem,
    e_send,
    e_recv,
    h_sem,
    s1_sem,
    m_sem,
    q_sem,
    n_send,
    n_recv,
    s2_sem,
):
    members, levels, child_rows, child_cols = child_ref.shape
    rows = child_rows // 3
    mem = lax.axis_index("mem")
    sx = lax.axis_index("sx")
    sy = lax.axis_index("sy")
    total_members = members * nmem
    here = {"mem": mem, "sx": sx, "sy": sy}

    loads = []
    for m in range(members):
        copy = pltpu.make_async_copy(child_ref.at[m], xbuf.at[m], ld_sem.at[m])
        copy.start()
        loads.append(copy)

    ring = nmem // 2
    z, y = mem // ring, lax.rem(mem, ring)
    steps = [(a, b) for b in (2, 1, 3, 0) for a in range(2) if (a, b) != (0, 0)]
    peers = [lax.rem(z + a, 2) * ring + lax.rem(y + b, ring) for a, b in steps]
    plane = [(a, b) for a in range(nsx) for b in range(nsy) if (a, b) != (0, 0)]
    plane_peers = [(lax.rem(sx + a, nsx), lax.rem(sy + b, nsy)) for a, b in plane]
    above, below = lax.rem(sx + 1, nsx), lax.rem(sx + nsx - 1, nsx)

    def at(m=None, x=None, y=None):
        return {
            "mem": here["mem"] if m is None else m,
            "sx": here["sx"] if x is None else x,
            "sy": here["sy"] if y is None else y,
        }

    def send(src, dst, pair, device):
        copy = pltpu.make_async_remote_copy(
            src_ref=src,
            dst_ref=dst,
            send_sem=pair[0],
            recv_sem=pair[1],
            device_id=device,
            device_id_type=MESH,
        )
        copy.start()

    def settle(ref, sem, received):
        copy = pltpu.make_async_remote_copy(
            src_ref=ref,
            dst_ref=ref,
            send_sem=sem,
            recv_sem=sem,
            device_id=at(m=peers[0]),
            device_id_type=MESH,
        )
        if received:
            copy.wait_recv()
        else:
            copy.wait_send()

    barrier = pltpu.get_barrier_semaphore()
    friends = [at(m=p) for p in peers]
    friends += [at(x=a, y=b) for a, b in plane_peers]
    friends += [at(m=p, x=x) for p in peers for x in (above, below)]
    for friend in friends:
        pl.semaphore_signal(barrier, inc=1, device_id=friend, device_id_type=MESH)

    zero = jnp.zeros((SUB, LANES), jnp.float32)

    def clear_slots(first):
        for slot in range(first, first + 2):
            for v in range(5):
                q[slot, v] = zero

    def clear_side(ref):
        for d in range(nmem):
            ref[d] = zero

    pl.when(sx == 0)(lambda: clear_slots(0))
    pl.when(sx == nsx - 1)(lambda: clear_slots(nmem + 2))
    pl.when(sy == 0)(lambda: clear_side(from_left))
    pl.when(sy == nsy - 1)(lambda: clear_side(from_right))

    r_ids = lax.broadcasted_iota(jnp.int32, (child_cols, child_cols // 3), 0)
    c_ids = lax.broadcasted_iota(jnp.int32, (child_cols, child_cols // 3), 1)
    off = r_ids - 3 * c_ids
    pick = jnp.where((off >= 0) & (off <= 2), 1.0, 0.0).astype(jnp.bfloat16)

    for m in range(members):
        loads[m].wait()
        wide = jnp.dot(
            xbuf[m].reshape(levels * child_rows, child_cols),
            pick,
            preferred_element_type=jnp.float32,
        )
        for c in range(2):
            ybuf[m % 2, c] = wide[:, c * LANES : (c + 1) * LANES]
        for i in range(rows):
            for c in range(2):
                total = ybuf[m % 2, c, pl.ds(3 * i, levels, stride=child_rows), :]
                for a in (1, 2):
                    total += ybuf[m % 2, c, pl.ds(3 * i + a, levels, stride=child_rows), :]
                psend[i // 2, m, 2 * c + i % 2] = total
        if m == 0:
            pl.semaphore_wait(barrier, len(friends))
        for n, p in enumerate(peers):
            send(psend.at[p, m], rbuf.at[n + 1, m], (p1_sem.at[0], p1_sem.at[1]), at(m=p))
        for v in range(4):
            rbuf[0, m, v] = psend[mem, m, v]

    lane = lax.broadcasted_iota(jnp.int32, (SUB, LANES), 1)
    for d in range(nmem):
        packed = zero
        for m in range(members):
            for i in range(2):
                shift = 8 * m + 64 * i
                both = jnp.where(lane < LANES // 2, psend[d, m, i], psend[d, m, 2 + i])
                if shift:
                    both = pltpu.roll(both, shift, 1)
                mine = ((lane - shift + 4 + LANES) & (LANES - 1)) < 8
                packed = jnp.where(mine, both, packed)
        pack[d] = packed

    @pl.when(sy < nsy - 1)
    def _():
        send(pack, from_left, (e_send.at[0], e_recv.at[0]), at(y=lax.rem(sy + 1, nsy)))

    @pl.when(sy > 0)
    def _():
        send(pack, from_right, (e_send.at[1], e_recv.at[1]), at(y=lax.rem(sy + nsy - 1, nsy)))

    pl.when(sy > 0)(lambda: settle(from_left, e_recv.at[0], True))
    pl.when(sy < nsy - 1)(lambda: settle(from_right, e_recv.at[1], True))
    for d in range(nmem):
        hsend[d] = jnp.where((lane & 4) == 0, from_right[d], from_left[d])
    for n, p in enumerate(peers):
        send(hsend.at[p], hbuf.at[n + 1], (h_sem.at[0], h_sem.at[1]), at(m=p))
    hbuf[0] = hsend[mem]

    settle(rbuf.at[pl.ds(1, nmem - 1)], p1_sem.at[1], True)

    def anomalies(v, var):
        total = zero
        for o in range(nmem):
            for m in range(members):
                total += rbuf[o, m, v]
        mean = total * (1.0 / total_members)
        mbuf[v] = mean * (1.0 / 9.0)
        for o in range(nmem):
            for m in range(members):
                anom = rbuf[o, m, v] - mean
                abuf[v, o * members + m] = anom
                var += anom * anom
        return var

    var = lax.fori_loop(0, 4, anomalies, zero)
    s1[0] = var
    for n, p in enumerate(peers):
        send(s1.at[0], s1.at[n + 1], (s1_sem.at[0], s1_sem.at[1]), at(m=p))
    for l in range(levels):
        mmsg[l] = zero
        for v in range(4):
            mmsg[l, pl.ds(v, 1), :] = mbuf[v, pl.ds(l, 1), :]
    for p in peers:
        send(mmsg.at[p], means.at[mem], (m_sem.at[0], m_sem.at[1]), at(m=p))
    means[mem] = mmsg[mem]

    settle(hbuf.at[pl.ds(1, nmem - 1)], h_sem.at[1], True)
    total = zero
    for o in range(nmem):
        for m in range(members):
            value = pltpu.roll(hbuf[o], LANES - 8 * m, 1) if m else hbuf[o]
            abuf[4, o * members + m] = value
            total += value
    mean = total * (1.0 / total_members)
    for t in range(total_members):
        abuf[4, t] = abuf[4, t] - mean

    factor = 1.0 / (81.0 * (total_members - 1))

    def covariances(v, carry):
        acc = [zero] * levels
        for t in range(total_members):
            anom = abuf[v, t]
            for l in range(levels):
                acc[l] += anom * abuf[v, t, pl.ds(l, 1), :]
        for l in range(levels):
            msg[l, v] = acc[l] * factor
        return carry

    lax.fori_loop(0, 5, covariances, 0)

    for p in peers:
        send(msg.at[p], q.at[mem + 2], (q_sem.at[0], q_sem.at[1]), at(m=p))
    sends_down = (mem < 2) & (sx > 0)
    sends_up = (mem >= nmem - 2) & (sx < nsx - 1)

    @pl.when(sends_down)
    def _():
        for l in range(levels):
            send(msg.at[l], q.at[mem + nmem + 2], (n_send.at[0], n_recv.at[1]), at(m=l, x=below))

    @pl.when(sends_up)
    def _():
        for l in range(levels):
            send(msg.at[l], q.at[mem - nmem + 2], (n_send.at[0], n_recv.at[0]), at(m=l, x=above))

    for v in range(5):
        q[mem + 2, v] = msg[mem, v]

    settle(s1.at[pl.ds(1, nmem - 1)], s1_sem.at[1], True)
    tile = s1[0]
    for o in range(1, nmem):
        tile += s1[o]
    s2[0] = tile
    for n, (a, b) in enumerate(plane_peers):
        send(s2.at[0], s2.at[n + 1], (s2_sem.at[0], s2_sem.at[1]), at(x=a, y=b))

    settle(means.at[pl.ds(0, nmem - 1)], m_sem.at[1], True)
    for d in range(nmem):
        means_ref[d] = means[d]
    settle(q.at[pl.ds(0, nmem - 1)], q_sem.at[1], True)
    pl.when(sx > 0)(lambda: settle(q.at[pl.ds(0, 2)], n_recv.at[0], True))
    pl.when(sx < nsx - 1)(lambda: settle(q.at[pl.ds(nmem + 2, 2)], n_recv.at[1], True))

    table = gaspari_table(REACH)

    for slot in range(nmem + 4):
        odd[slot] = pltpu.roll(q[slot, 4], LANES // 2, 1)

    def cells(i):
        slot, i2 = i // 2, i % 2
        side = odd[slot] if i2 else q[slot, 4]
        return jnp.concatenate([q[slot, i2], q[slot, 2 + i2], side], axis=1)

    for i in range(rows):
        center = i + REACH
        lines = [cells(center)]
        for e in range(1, REACH + 1):
            lines.append(cells(center - e) + cells(center + e))
        out = None
        for f in range(REACH + 1):
            line = None
            for e in range(REACH + 1):
                weight = float(table[REACH + e, REACH + f])
                if weight != 0.0:
                    term = weight * lines[e]
                    line = term if line is None else line + term
            if f == 0:
                out = line
            else:
                width = 3 * LANES
                out = out + pltpu.roll(line, f, 1) + pltpu.roll(line, width - f, 1)
        for c in range(2):
            z_ref[c, pl.ds(i, levels, stride=rows), :] = out[:, c * LANES : (c + 1) * LANES]

    settle(s2.at[pl.ds(1, len(plane))], s2_sem.at[1], True)
    everyone = s2[0]
    for n in range(len(plane)):
        everyone += s2[n + 1]
    all_ref[...] = everyone

    settle(psend.at[pl.ds(0, nmem - 1)], p1_sem.at[0], False)
    pl.when(sy < nsy - 1)(lambda: settle(pack, e_send.at[0], False))
    pl.when(sy > 0)(lambda: settle(pack, e_send.at[1], False))
    settle(hsend.at[pl.ds(0, nmem - 1)], h_sem.at[0], False)
    settle(s1.at[pl.ds(0, nmem - 1)], s1_sem.at[0], False)
    settle(mmsg.at[pl.ds(0, nmem - 1)], m_sem.at[0], False)
    settle(msg.at[pl.ds(0, nmem - 1)], q_sem.at[0], False)
    pl.when(sends_down | sends_up)(lambda: settle(msg, n_send.at[0], False))
    settle(s2.at[pl.ds(0, len(plane))], s2_sem.at[0], False)


def scale(count, z_ref, all_ref, means_ref, mean_ref, cov_ref):
    levels, rows, cols = cov_ref.shape
    spread = jnp.sum(all_ref[...], keepdims=True) * (1.0 / count)
    inverse = 1.0 / (spread + 1e-6)
    for k in range(levels):
        for c in range(cols // LANES):
            block = z_ref[c, pl.ds(k * rows, rows), :]
            cov_ref[k, :, pl.ds(c * LANES, LANES)] = block * inverse
    for i in range(rows):
        for c in range(cols // LANES):
            row = means_ref[i // 2, pl.ds(2 * c + i % 2, 1), :]
            mean_ref[0, pl.ds(i, 1), pl.ds(c * LANES, LANES)] = row


def solution(mesh):
    nmem, nsx, nsy = (mesh.shape[name] for name in ("mem", "sx", "sy"))

    def local(child):
        members, levels, child_rows, child_cols = child.shape
        rows, cols = child_rows // 3, child_cols // 3
        f32 = jnp.float32
        dma = pltpu.SemaphoreType.DMA
        vmem = pl.BlockSpec(memory_space=pltpu.VMEM)
        vector = (SUB, LANES)
        z, total, means = pl.pallas_call(
            functools.partial(gather, nmem, nsx, nsy),
            out_shape=(
                jax.ShapeDtypeStruct((2, levels * rows, LANES), f32),
                jax.ShapeDtypeStruct(vector, f32),
                jax.ShapeDtypeStruct((nmem, *vector), f32),
            ),
            in_specs=[pl.BlockSpec(memory_space=pltpu.MemorySpace.HBM)],
            out_specs=(vmem, vmem, vmem),
            scratch_shapes=[
                pltpu.VMEM(child.shape, child.dtype),
                pltpu.VMEM((2, 2, levels * child_rows, LANES), f32),
                pltpu.VMEM((nmem, members, 4, *vector), f32),
                pltpu.VMEM((nmem, members, 4, *vector), f32),
                pltpu.VMEM((nmem, *vector), f32),
                pltpu.VMEM((nmem, *vector), f32),
                pltpu.VMEM((nmem, *vector), f32),
                pltpu.VMEM((nmem, *vector), f32),
                pltpu.VMEM((nmem, *vector), f32),
                pltpu.VMEM((5, nmem * members, *vector), f32),
                pltpu.VMEM((4, *vector), f32),
                pltpu.VMEM((levels, *vector), f32),
                pltpu.VMEM((nmem, *vector), f32),
                pltpu.VMEM((levels, 5, *vector), f32),
                pltpu.VMEM((nmem + 4, 5, *vector), f32),
                pltpu.VMEM((nmem + 4, *vector), f32),
                pltpu.VMEM((nmem, *vector), f32),
                pltpu.VMEM((nsx * nsy, *vector), f32),
                dma((members,)),
                dma((2,)),
                dma((2,)),
                dma((2,)),
                dma((2,)),
                dma((2,)),
                dma((2,)),
                dma((2,)),
                dma((1,)),
                dma((2,)),
                dma((2,)),
            ],
            compiler_params=pltpu.CompilerParams(collective_id=0, has_side_effects=True, vmem_limit_bytes=VMEM_GRANT),
            name="gather",
        )(child)
        count = 81.0 * (members * nmem - 1) * levels * rows * nsx * cols * nsy
        return pl.pallas_call(
            functools.partial(scale, count),
            out_shape=(
                jax.ShapeDtypeStruct((levels // nmem, rows, cols), f32),
                jax.ShapeDtypeStruct((levels, rows, cols), f32),
            ),
            in_specs=[vmem, vmem, vmem],
            out_specs=(vmem, vmem),
            compiler_params=pltpu.CompilerParams(vmem_limit_bytes=8 << 20),
            name="scale",
        )(z, total, means)

    return jax.shard_map(
        local,
        mesh=mesh,
        in_specs=(P("mem", None, "sx", "sy"),),
        out_specs=(P("mem", "sx", "sy"), P("mem", "sx", "sy")),
        check_vma=False,
    )
```

time: 196 us -> 28.8 us (0.15); the launches traced: 193 us -> 28.7 us
  other arithmetic: 56.4 us -> 0 us
  local copies, waits for them, and re-layouts: 50 us -> 0 us
  blocking collectives: 31.8 us -> 0 us
  Pallas kernels: 0 us -> 28.1 us
  starting transfers between devices: 23.7 us -> 0 us
  matrix products: 14.8 us -> 0 us
  waiting for transfers between devices: 14.6 us -> 0 us
    reduce_sum x5 -> x0, other arithmetic: 53.5 us -> none  [the longest x1 42.6 us: local(): jnp.sum(child.reshape(members_dev, levels, rows_dev, 3, cols_dev, 3), axi...]
    convert_element_type x1 -> x0, local copies, waits for them, and re-layouts: 37.3 us -> none  [local(): jnp.sum(child.reshape(members_dev, levels, rows_dev, 3, cols_dev, 3), axi...]
    psum x5 -> x0, blocking collectives: 31.8 us -> none  [one_axis_at_a_time(): array = lax.psum(array, axis)]
    pallas_call x0 -> x2, Pallas kernels: none -> 28.1 us  [the longest x1 27.3 us: local(): pl.pallas_call(functools.partial(gather, nmem, nsx, nsy), out_shape=(jax....]
    dot_general x1 -> x0, matrix products: 14.8 us -> none  [local(): jnp.einsum('alxy,akxy->lkxy', parent, parent)]
    all_to_all x2 -> x0, waiting for transfers between devices: 14.6 us -> none  [the longest x1 14.6 us: sum_at_owner(): lax.all_to_all(cut_along(array, dim, devices), axis, 0, 0, tiled=True)]
    ppermute x4 -> x0, starting transfers between devices: 12.2 us -> none  [the longest x2 8.23 us: padded_2(): before = lax.ppermute(last, axis, up)]
    all_to_all x2 -> x0, starting transfers between devices: 11.5 us -> none  [the longest x1 6.36 us: from_everyone(): return lax.all_to_all(copies, axis, split_axis=0, concat_axis=0, tiled=True)]
  transfers between devices with their start and end apart: 6 -> 0, of which waited for: 1 -> 0; matrix products, arithmetic and copies ran while one was open for 13% -> 0% of each run, Pallas kernels for 0% -> 0%
where the time goes in v2:
time: 28.8 us; the launch traced here: 28.7 us
  Pallas kernels  28.1 us (98%)
  between operations  0.64 us (2%)
    pallas_call x1, Pallas kernels, local(): pl.pallas_call(functools.partial(gather, nmem, nsx, nsy), out_shape=(jax....  27.3 us
    pallas_call x1, Pallas kernels, local(): pl.pallas_call(functools.partial(scale, count), out_shape=(jax.ShapeDtype...  0.79 us

profile of v2, /device:TPU:1, one launch (start us, length us, event | category | flops | bytes accessed | tf_op | source)
XLA Modules:
  0.0 28.7 jit_solution(9887659643803210961)
XLA Ops:
  0.6 27.3 %gather.1 = (f32[2,128,128]{2,1,0:T(8,128)S(1)}, f32[8,128]{1,0:T(8,128)S(1)}, f32[8,8,128]{2,1,0:T(8,128)S(1)}) custom-call(bf16[4,8,48,768]{3,2,1,0:T(8,128)(2,1)} %child_ref.1), custom_call_target="tpu_custom_call" | custom-call | tf_op jit(solution)/shard_map/gather/pallas_call | solution.py:365
  27.9 0.8 %scale.1 = (f32[1,16,256]{2,1,0:T(8,128)}, f32[8,16,256]{2,1,0:T(8,128)}) custom-call(f32[2,128,128]{2,1,0:T(8,128)S(1)} %get-tuple-element.5.z_ref, f32[8,128]{1,0:T(8,128)S(1)} %get-tuple-element.6.all_ref, f32[8,8,128]{2,1,0:T(8,128)S(1)} %get-tuple-element.7.means_ref), custom_call_target="tpu_custom_call" | custom-call | tf_op jit(solution)/shard_map/scale/pallas_call | solution.py:409

commit v3 on v2

v3 whole, which is shorter than its diff:
```python
import functools

import jax
import jax.numpy as jnp
import numpy as np
from jax import lax
from jax.experimental import pallas as pl
from jax.experimental.pallas import tpu as pltpu
from jax.sharding import PartitionSpec as P

MESH = pl.DeviceIdType.MESH
REACH = 4
LANES = 128
SUB = 8
VMEM_GRANT = 55_500_000


def gaspari_table(reach):
    offsets = np.arange(-reach, reach + 1) * 1.0
    dist = np.sqrt(offsets[:, None] ** 2 + offsets[None, :] ** 2) / 2.5
    near = -0.25 * dist**5 + 0.5 * dist**4 + 0.625 * dist**3 - 5.0 / 3.0 * dist**2 + 1.0
    safe = np.maximum(dist, 0.001)
    far = (
        dist**5 / 12.0
        - 0.5 * dist**4
        + 0.625 * dist**3
        + 5.0 / 3.0 * dist**2
        - 5.0 * dist
        + 4.0
        - 2.0 / (3.0 * safe)
    )
    table = np.where(dist <= 1.0, near, np.where(dist < 2.0, far, 0.0))
    return table / table.sum()


def gather(
    nmem,
    nsx,
    nsy,
    child_ref,
    z_ref,
    all_ref,
    means_ref,
    xbuf,
    pick,
    ybuf,
    psend,
    rbuf,
    pack,
    from_left,
    from_right,
    hsend,
    hbuf,
    abuf,
    sbuf,
    mbuf,
    mmsg,
    means,
    msg,
    q,
    odd,
    s1,
    s2,
    ld_sem,
    p1_sem,
    e_send,
    e_recv,
    h_sem,
    s1_sem,
    m_sem,
    q_sem,
    n_send,
    n_recv,
    s2_sem,
):
    members, levels, child_rows, child_cols = child_ref.shape
    rows = child_rows // 3
    half_rows = child_rows // 2
    mem = lax.axis_index("mem")
    sx = lax.axis_index("sx")
    sy = lax.axis_index("sy")
    total_members = members * nmem
    ring = nmem // 2
    z, y = mem // ring, lax.rem(mem, ring)

    def at(m=None, x=None, y=None):
        return {
            "mem": mem if m is None else m,
            "sx": sx if x is None else x,
            "sy": sy if y is None else y,
        }

    loads = []
    for half, owner_z in enumerate((1 - z, z)):
        first = pl.multiple_of(owner_z * half_rows, SUB)
        copy = pltpu.make_async_copy(
            child_ref.at[:, :, pl.ds(first, half_rows), :], xbuf.at[half], ld_sem.at[half]
        )
        copy.start()
        loads.append(copy)

    steps = [(1, 0), (1, 1), (1, 3), (1, 2), (0, 2), (0, 1), (0, 3)]
    spots = [lax.rem(y + b, ring) for _, b in steps]
    peers = [lax.rem(z + a, 2) * ring + spot for (a, _), spot in zip(steps, spots)]
    plane = [(a, b) for a in range(nsx) for b in range(nsy) if (a, b) != (0, 0)]
    plane_peers = [(lax.rem(sx + a, nsx), lax.rem(sy + b, nsy)) for a, b in plane]
    above, below = lax.rem(sx + 1, nsx), lax.rem(sx + nsx - 1, nsx)

    def send(src, dst, pair, device):
        copy = pltpu.make_async_remote_copy(
            src_ref=src,
            dst_ref=dst,
            send_sem=pair[0],
            recv_sem=pair[1],
            device_id=device,
            device_id_type=MESH,
        )
        copy.start()

    def settle(ref, sem, received):
        copy = pltpu.make_async_remote_copy(
            src_ref=ref,
            dst_ref=ref,
            send_sem=sem,
            recv_sem=sem,
            device_id=at(m=peers[0]),
            device_id_type=MESH,
        )
        if received:
            copy.wait_recv()
        else:
            copy.wait_send()

    barrier = pltpu.get_barrier_semaphore()
    friends = [at(m=p) for p in peers]
    friends += [at(x=a, y=b) for a, b in plane_peers]
    friends += [at(m=p, x=x) for p in peers for x in (above, below)]
    for friend in friends:
        pl.semaphore_signal(barrier, inc=1, device_id=friend, device_id_type=MESH)

    zero = jnp.zeros((SUB, LANES), jnp.float32)

    width = 3 * LANES
    r_ids = lax.broadcasted_iota(jnp.int32, (width, LANES), 0)
    c_ids = lax.broadcasted_iota(jnp.int32, (width, LANES), 1)
    off = r_ids - 3 * c_ids
    pick[...] = jnp.where((off >= 0) & (off <= 2), 1.0, 0.0).astype(jnp.bfloat16)

    def post(first, count, n, sem):
        part = pl.ds(first, count)
        send(
            psend.at[1 - steps[n][0], spots[n], part],
            rbuf.at[n + 1, part],
            (p1_sem.at[0], p1_sem.at[sem]),
            at(m=peers[n]),
        )

    within = zero
    for half, owner_z in enumerate((1 - z, z)):
        loads[half].wait()
        for c in range(2):
            ybuf[c] = jnp.dot(
                xbuf[half, :, :, :, pl.ds(c * width, width)].reshape(-1, width),
                pick[...],
                preferred_element_type=jnp.float32,
            )
        for i in range(rows // 2):
            for c in range(2):
                p = []
                for m in range(members):
                    total = None
                    for a in range(3):
                        start = m * levels * half_rows + 3 * i + a
                        line = ybuf[c, pl.ds(start, levels, stride=half_rows), :]
                        total = line if total is None else total + line
                    p.append(total)
                up, down = p[0] + p[1], p[2] + p[3]
                left, right = p[0] - p[1], p[2] - p[3]
                owner, inside = i % ring, i // ring
                i2 = inside + owner_z - 2 * inside * owner_z
                psend[half, owner, 2 * i2 + c] = up + down
                for j, value in enumerate((up - down, left + right, left - right)):
                    psend[half, owner, 4 + 6 * i2 + 2 * j + c] = value
                    within += value * value
        if half == 0:
            pl.semaphore_wait(barrier, len(friends))
            for n in range(ring):
                post(0, 4, n, 1)
            post(4, 6, 0, 2)
        else:
            for n in range(ring, nmem - 1):
                post(0, 4, n, 1)
            for n in range(1, nmem - 1):
                post(4, 6, n, 2)
    for k in range(16):
        rbuf[0, k] = psend[1, y, k]

    def clear_rows(first):
        for row in range(first, first + REACH):
            for v in range(3):
                q[row, v] = zero

    def clear_side(ref):
        for d in range(nmem):
            ref[d] = zero

    pl.when(sx == 0)(lambda: clear_rows(0))
    pl.when(sx == nsx - 1)(lambda: clear_rows(REACH + rows))
    pl.when(sy == 0)(lambda: clear_side(from_left))
    pl.when(sy == nsy - 1)(lambda: clear_side(from_right))

    lane = lax.broadcasted_iota(jnp.int32, (SUB, LANES), 1)
    for d in range(nmem):
        half, owner = d // ring, d % ring
        packed = zero
        for j in range(members):
            for i2 in range(2):
                shift = 8 * j + 64 * i2
                k = 2 * i2 if j == 0 else 2 + 6 * i2 + 2 * j
                both = jnp.where(
                    lane < LANES // 2, psend[half, owner, k], psend[half, owner, k + 1]
                )
                if shift:
                    both = pltpu.roll(both, shift, 1)
                mine = ((lane - shift + 4 + LANES) & (LANES - 1)) < 8
                packed = jnp.where(mine, both, packed)
        pack[d] = packed

    @pl.when(sy < nsy - 1)
    def _():
        send(pack, from_left, (e_send.at[0], e_recv.at[0]), at(y=lax.rem(sy + 1, nsy)))

    @pl.when(sy > 0)
    def _():
        send(pack, from_right, (e_send.at[1], e_recv.at[1]), at(y=lax.rem(sy + nsy - 1, nsy)))

    pl.when(sy > 0)(lambda: settle(from_left, e_recv.at[0], True))
    pl.when(sy < nsy - 1)(lambda: settle(from_right, e_recv.at[1], True))
    for d in range(nmem):
        hsend[d] = jnp.where((lane & 4) == 0, from_right[d], from_left[d])
    for n, (p, spot) in enumerate(zip(peers, spots)):
        send(
            hsend.at[(1 - steps[n][0]) * ring + spot],
            hbuf.at[n + 1],
            (h_sem.at[0], h_sem.at[1]),
            at(m=p),
        )
    hbuf[0] = hsend[ring + y]

    settle(rbuf.at[pl.ds(1, nmem - 1), pl.ds(0, 4)], p1_sem.at[1], True)
    var = within
    for v in range(4):
        total = rbuf[0, v]
        for o in range(1, nmem):
            total += rbuf[o, v]
        mbuf[v] = total * (1.0 / (9.0 * total_members))
        middle = total * (1.0 / nmem)
        for o in range(nmem):
            anom = rbuf[o, v] - middle
            abuf[v, o] = anom
            var += anom * anom
    s1[0] = var
    for n, p in enumerate(peers):
        send(s1.at[0], s1.at[n + 1], (s1_sem.at[0], s1_sem.at[1]), at(m=p))
    for n in range(nmem - 1):
        post(10, 6, n, 3)
    for l in range(levels):
        mmsg[l] = zero
        for v in range(4):
            mmsg[l, pl.ds(v, 1), :] = mbuf[v, pl.ds(l, 1), :]
    for p in peers:
        send(mmsg.at[p], means.at[mem], (m_sem.at[0], m_sem.at[1]), at(m=p))
    means[mem] = mmsg[mem]

    factor = 1.0 / (4.0 * 81.0 * (total_members - 1))

    def covariances(v, vectors):
        acc = [zero] * levels
        for ref, index in vectors:
            anom = ref[index]
            for l in range(levels):
                acc[l] += anom * ref[(*index, pl.ds(l, 1), slice(None))]
        for l in range(levels):
            msg[l, v] = acc[l] * factor

    def cells_of_row(i2, first):
        def column(c, carry):
            vectors = []
            for o in range(nmem):
                vectors.append((abuf, (2 * i2 + c, o)))
                vectors += [(rbuf, (o, 4 + 6 * i2 + 2 * j + c)) for j in range(members - 1)]
            covariances(first + c, vectors)
            return carry

        lax.fori_loop(0, 2, column, 0)

    settle(rbuf.at[pl.ds(1, nmem - 1), pl.ds(4, 6)], p1_sem.at[2], True)
    cells_of_row(0, 0)
    settle(hbuf.at[pl.ds(1, nmem - 1)], h_sem.at[1], True)
    total = hbuf[0]
    for o in range(1, nmem):
        total += hbuf[o]
    middle = total * (1.0 / nmem)
    for o in range(nmem):
        sbuf[members * o] = hbuf[o] - middle
        for j in range(1, members):
            sbuf[members * o + j] = pltpu.roll(hbuf[o], LANES - 8 * j, 1)
    covariances(2, [(sbuf, (t,)) for t in range(total_members)])

    edge_row = mem + z * (rows - nmem)
    sends_down = (z == 0) & (sx > 0)
    sends_up = (z == 1) & (sx < nsx - 1)
    edge_part, inner_part = pl.ds(0, 3), pl.ds(3, 2)

    @pl.when(sends_down)
    def _():
        for l in range(levels):
            pair = (n_send.at[0], n_recv.at[1])
            row = REACH + rows + mem
            send(msg.at[l, edge_part], q.at[row], pair, at(m=l, x=below))

    @pl.when(sends_up)
    def _():
        for l in range(levels):
            pair = (n_send.at[0], n_recv.at[0])
            row = mem - ring
            send(msg.at[l, edge_part], q.at[row], pair, at(m=l, x=above))

    for p in peers:
        pair = (q_sem.at[0], q_sem.at[1])
        send(msg.at[p, edge_part], q.at[REACH + edge_row], pair, at(m=p))
    for v in range(3):
        q[REACH + edge_row, v] = msg[mem, v]

    settle(s1.at[pl.ds(1, nmem - 1)], s1_sem.at[1], True)
    tile = s1[0]
    for o in range(1, nmem):
        tile += s1[o]
    s2[0] = tile
    for n, (a, b) in enumerate(plane_peers):
        send(s2.at[0], s2.at[n + 1], (s2_sem.at[0], s2_sem.at[1]), at(x=a, y=b))

    settle(rbuf.at[pl.ds(1, nmem - 1), pl.ds(10, 6)], p1_sem.at[3], True)
    cells_of_row(1, 3)
    inner_row = REACH + mem
    for p in peers:
        pair = (q_sem.at[0], q_sem.at[1])
        send(msg.at[p, inner_part], q.at[REACH + inner_row, pl.ds(0, 2)], pair, at(m=p))
    for v in range(2):
        q[REACH + inner_row, v] = msg[mem, 3 + v]

    settle(means.at[pl.ds(0, nmem - 1)], m_sem.at[1], True)
    for d in range(nmem):
        means_ref[d] = means[d]
    settle(msg.at[pl.ds(0, nmem - 1)], q_sem.at[1], True)
    pl.when(sx > 0)(lambda: settle(q.at[pl.ds(0, REACH)], n_recv.at[0], True))
    pl.when(sx < nsx - 1)(lambda: settle(q.at[pl.ds(REACH + rows, REACH)], n_recv.at[1], True))

    table = gaspari_table(REACH)
    for d in range(nmem):
        row = d if d < ring else d + rows - nmem
        odd[d] = pltpu.roll(q[REACH + row, 2], LANES // 2, 1)

    def cells(row):
        inner = row - 2 * REACH
        side = odd[inner] if 0 <= inner < nmem else q[row, 2]
        return jnp.concatenate([q[row, 0], q[row, 1], side], axis=1)

    for i in range(rows):
        center = i + REACH
        lines = [cells(center)]
        for e in range(1, REACH + 1):
            lines.append(cells(center - e) + cells(center + e))
        out = None
        for f in range(REACH + 1):
            line = None
            for e in range(REACH + 1):
                weight = float(table[REACH + e, REACH + f])
                if weight != 0.0:
                    term = weight * lines[e]
                    line = term if line is None else line + term
            if f == 0:
                out = line
            else:
                out = out + pltpu.roll(line, f, 1) + pltpu.roll(line, width - f, 1)
        for c in range(2):
            z_ref[c, pl.ds(i, levels, stride=rows), :] = out[:, c * LANES : (c + 1) * LANES]

    settle(s2.at[pl.ds(1, len(plane))], s2_sem.at[1], True)
    everyone = s2[0]
    for n in range(len(plane)):
        everyone += s2[n + 1]
    all_ref[...] = everyone

    settle(rbuf.at[pl.ds(1, nmem - 1)], p1_sem.at[0], False)
    pl.when(sy < nsy - 1)(lambda: settle(pack, e_send.at[0], False))
    pl.when(sy > 0)(lambda: settle(pack, e_send.at[1], False))
    settle(hsend.at[pl.ds(0, nmem - 1)], h_sem.at[0], False)
    settle(s1.at[pl.ds(0, nmem - 1)], s1_sem.at[0], False)
    settle(mmsg.at[pl.ds(0, nmem - 1)], m_sem.at[0], False)
    settle(msg.at[pl.ds(0, nmem - 1)], q_sem.at[0], False)
    pl.when(sends_down | sends_up)(lambda: settle(q.at[pl.ds(0, levels)], n_send.at[0], False))
    settle(s2.at[pl.ds(0, len(plane))], s2_sem.at[0], False)


def scale(count, z_ref, all_ref, means_ref, mean_ref, cov_ref):
    levels, rows, cols = cov_ref.shape
    spread = jnp.sum(all_ref[...], keepdims=True) * (1.0 / count)
    inverse = 1.0 / (spread + 1e-6)
    for k in range(levels):
        for c in range(cols // LANES):
            block = z_ref[c, pl.ds(k * rows, rows), :]
            cov_ref[k, :, pl.ds(c * LANES, LANES)] = block * inverse
    for i in range(rows):
        inner = 1 if REACH <= i < rows - REACH else 0
        source = i - REACH if inner else i % (rows - 2 * REACH)
        for c in range(cols // LANES):
            row = means_ref[source, pl.ds(2 * inner + c, 1), :]
            mean_ref[0, pl.ds(i, 1), pl.ds(c * LANES, LANES)] = row


def solution(mesh):
    nmem, nsx, nsy = (mesh.shape[name] for name in ("mem", "sx", "sy"))

    def local(child):
        members, levels, child_rows, child_cols = child.shape
        rows, cols = child_rows // 3, child_cols // 3
        f32 = jnp.float32
        dma = pltpu.SemaphoreType.DMA
        vmem = pl.BlockSpec(memory_space=pltpu.VMEM)
        vector = (SUB, LANES)
        z, total, means = pl.pallas_call(
            functools.partial(gather, nmem, nsx, nsy),
            out_shape=(
                jax.ShapeDtypeStruct((2, levels * rows, LANES), f32),
                jax.ShapeDtypeStruct(vector, f32),
                jax.ShapeDtypeStruct((nmem, *vector), f32),
            ),
            in_specs=[pl.BlockSpec(memory_space=pltpu.MemorySpace.HBM)],
            out_specs=(vmem, vmem, vmem),
            scratch_shapes=[
                pltpu.VMEM((2, members, levels, child_rows // 2, child_cols), child.dtype),
                pltpu.VMEM((3 * LANES, LANES), child.dtype),
                pltpu.VMEM((2, members * levels * child_rows // 2, LANES), f32),
                pltpu.VMEM((2, nmem // 2, 16, *vector), f32),
                pltpu.VMEM((nmem, 16, *vector), f32),
                pltpu.VMEM((nmem, *vector), f32),
                pltpu.VMEM((nmem, *vector), f32),
                pltpu.VMEM((nmem, *vector), f32),
                pltpu.VMEM((nmem, *vector), f32),
                pltpu.VMEM((nmem, *vector), f32),
                pltpu.VMEM((4, nmem, *vector), f32),
                pltpu.VMEM((nmem * members, *vector), f32),
                pltpu.VMEM((4, *vector), f32),
                pltpu.VMEM((levels, *vector), f32),
                pltpu.VMEM((nmem, *vector), f32),
                pltpu.VMEM((levels, 5, *vector), f32),
                pltpu.VMEM((rows + 2 * REACH, 3, *vector), f32),
                pltpu.VMEM((nmem, *vector), f32),
                pltpu.VMEM((nmem, *vector), f32),
                pltpu.VMEM((nsx * nsy, *vector), f32),
                dma((2,)),
                dma((4,)),
                dma((2,)),
                dma((2,)),
                dma((2,)),
                dma((2,)),
                dma((2,)),
                dma((2,)),
                dma((1,)),
                dma((2,)),
                dma((2,)),
            ],
            compiler_params=pltpu.CompilerParams(collective_id=0, has_side_effects=True, vmem_limit_bytes=VMEM_GRANT),
            name="gather",
        )(child)
        count = 4.0 * 81.0 * (members * nmem - 1) * levels * rows * nsx * cols * nsy
        return pl.pallas_call(
            functools.partial(scale, count),
            out_shape=(
                jax.ShapeDtypeStruct((levels // nmem, rows, cols), f32),
                jax.ShapeDtypeStruct((levels, rows, cols), f32),
            ),
            in_specs=[vmem, vmem, vmem],
            out_specs=(vmem, vmem),
            compiler_params=pltpu.CompilerParams(vmem_limit_bytes=8 << 20),
            name="scale",
        )(z, total, means)

    return jax.shard_map(
        local,
        mesh=mesh,
        in_specs=(P("mem", None, "sx", "sy"),),
        out_specs=(P("mem", "sx", "sy"), P("mem", "sx", "sy")),
        check_vma=False,
    )
```

time: 28.8 us -> 24.2 us (0.84)
  the two profiles are of different devices: /device:TPU:1 before, /device:TPU:0 now
where the time goes in v3:
time: 24.2 us; the launch traced here: 24.1 us
  Pallas kernels  23.4 us (97%)
  between operations  0.64 us (3%)
    pallas_call x1, Pallas kernels, local(): pl.pallas_call(functools.partial(gather, nmem, nsx, nsy), out_shape=(jax....  22.7 us
    pallas_call x1, Pallas kernels, local(): pl.pallas_call(functools.partial(scale, count), out_shape=(jax.ShapeDtype...  0.79 us

profile of v3, /device:TPU:0, one launch (start us, length us, event | category | flops | bytes accessed | tf_op | source)
XLA Modules:
  0.0 24.1 jit_solution(13593012474331698008)
XLA Ops:
  0.6 22.7 %gather.1 = (f32[2,128,128]{2,1,0:T(8,128)S(1)}, f32[8,128]{1,0:T(8,128)S(1)}, f32[8,8,128]{2,1,0:T(8,128)S(1)}) custom-call(bf16[4,8,48,768]{3,2,1,0:T(8,128)(2,1)} %child_ref.1), custom_call_target="tpu_custom_call" | custom-call | tf_op jit(solution)/shard_map/gather/pallas_call | solution.py:432
  23.3 0.8 %scale.1 = (f32[1,16,256]{2,1,0:T(8,128)}, f32[8,16,256]{2,1,0:T(8,128)}) custom-call(f32[2,128,128]{2,1,0:T(8,128)S(1)} %get-tuple-element.5.z_ref, f32[8,128]{1,0:T(8,128)S(1)} %get-tuple-element.6.all_ref, f32[8,8,128]{2,1,0:T(8,128)S(1)} %get-tuple-element.7.means_ref), custom_call_target="tpu_custom_call" | custom-call | tf_op jit(solution)/shard_map/scale/pallas_call | solution.py:478

commit v4 on v3

--- a/solution.py
+++ b/solution.py
@@ -72,6 +72,7 @@
     n_send,
     n_recv,
     s2_sem,
+    known,
 ):
     members, levels, child_rows, child_cols = child_ref.shape
     rows = child_rows // 3
@@ -131,12 +132,24 @@
         else:
             copy.wait_send()
 
+    def greet(sem, friend):
+        pl.semaphore_signal(sem, inc=1, device_id=friend, device_id_type=MESH)
+
+    def greet_around(sem):
+        for a in (-1, 0, 1):
+            for b in (-1, 0, 1):
+                if (a, b) != (0, 0):
+                    inside = (sx + a >= 0) & (sx + a < nsx) & (sy + b >= 0) & (sy + b < nsy)
+                    friend = at(x=lax.rem(sx + a + nsx, nsx), y=lax.rem(sy + b + nsy, nsy))
+                    pl.when(inside)(lambda: greet(sem, friend))
+
+    tiles_x = 3 - jnp.where(sx == 0, 1, 0) - jnp.where(sx == nsx - 1, 1, 0)
+    tiles_y = 3 - jnp.where(sy == 0, 1, 0) - jnp.where(sy == nsy - 1, 1, 0)
+    around = tiles_x * tiles_y - 1
     barrier = pltpu.get_barrier_semaphore()
-    friends = [at(m=p) for p in peers]
-    friends += [at(x=a, y=b) for a, b in plane_peers]
-    friends += [at(m=p, x=x) for p in peers for x in (above, below)]
-    for friend in friends:
-        pl.semaphore_signal(barrier, inc=1, device_id=friend, device_id_type=MESH)
+    for p in peers:
+        greet(barrier, at(m=p))
+    greet_around(barrier)
 
     zero = jnp.zeros((SUB, LANES), jnp.float32)
 
@@ -182,19 +195,6 @@
                 for j, value in enumerate((up - down, left + right, left - right)):
                     psend[half, owner, 4 + 6 * i2 + 2 * j + c] = value
                     within += value * value
-        if half == 0:
-            pl.semaphore_wait(barrier, len(friends))
-            for n in range(ring):
-                post(0, 4, n, 1)
-            post(4, 6, 0, 2)
-        else:
-            for n in range(ring, nmem - 1):
-                post(0, 4, n, 1)
-            for n in range(1, nmem - 1):
-                post(4, 6, n, 2)
-    for k in range(16):
-        rbuf[0, k] = psend[1, y, k]
-
     def clear_rows(first):
         for row in range(first, first + REACH):
             for v in range(3):
@@ -226,6 +226,11 @@
                 packed = jnp.where(mine, both, packed)
         pack[d] = packed
 
+    pl.semaphore_wait(barrier, len(peers) + around)
+    greet_around(known.at[0])
+    for n in (3, 1, 2, 4, 0, 5, 6):
+        post(0, 4, n, 1)
+
     @pl.when(sy < nsy - 1)
     def _():
         send(pack, from_left, (e_send.at[0], e_recv.at[0]), at(y=lax.rem(sy + 1, nsy)))
@@ -233,6 +238,13 @@
     @pl.when(sy > 0)
     def _():
         send(pack, from_right, (e_send.at[1], e_recv.at[1]), at(y=lax.rem(sy + nsy - 1, nsy)))
+
+    for n in range(nmem - 1):
+        post(4, 6, n, 2)
+    for n in range(0):
+        post(10, 6, n, 3)
+    for k in range(16):
+        rbuf[0, k] = psend[1, y, k]
 
     pl.when(sy > 0)(lambda: settle(from_left, e_recv.at[0], True))
     pl.when(sy < nsy - 1)(lambda: settle(from_right, e_recv.at[1], True))
@@ -247,6 +259,9 @@
         )
     hbuf[0] = hsend[ring + y]
 
+    pl.semaphore_wait(known.at[0], around)
+    greet_around(known.at[1])
+
     settle(rbuf.at[pl.ds(1, nmem - 1), pl.ds(0, 4)], p1_sem.at[1], True)
     var = within
     for v in range(4):
@@ -259,7 +274,7 @@
             anom = rbuf[o, v] - middle
             abuf[v, o] = anom
             var += anom * anom
-    s1[0] = var
+    s1[0] = jnp.sum(var, axis=0, keepdims=True)
     for n, p in enumerate(peers):
         send(s1.at[0], s1.at[n + 1], (s1_sem.at[0], s1_sem.at[1]), at(m=p))
     for n in range(nmem - 1):
@@ -333,10 +348,8 @@
         q[REACH + edge_row, v] = msg[mem, v]
 
     settle(s1.at[pl.ds(1, nmem - 1)], s1_sem.at[1], True)
-    tile = s1[0]
-    for o in range(1, nmem):
-        tile += s1[o]
-    s2[0] = tile
+    pl.semaphore_wait(known.at[1], around)
+    s2[0] = jnp.sum(s1[...], axis=0)
     for n, (a, b) in enumerate(plane_peers):
         send(s2.at[0], s2.at[n + 1], (s2_sem.at[0], s2_sem.at[1]), at(x=a, y=b))
 
@@ -387,10 +400,7 @@
             z_ref[c, pl.ds(i, levels, stride=rows), :] = out[:, c * LANES : (c + 1) * LANES]
 
     settle(s2.at[pl.ds(1, len(plane))], s2_sem.at[1], True)
-    everyone = s2[0]
-    for n in range(len(plane)):
-        everyone += s2[n + 1]
-    all_ref[...] = everyone
+    all_ref[...] = jnp.sum(s2[...], axis=0)
 
     settle(rbuf.at[pl.ds(1, nmem - 1)], p1_sem.at[0], False)
     pl.when(sy < nsy - 1)(lambda: settle(pack, e_send.at[0], False))
@@ -433,7 +443,7 @@
             functools.partial(gather, nmem, nsx, nsy),
             out_shape=(
                 jax.ShapeDtypeStruct((2, levels * rows, LANES), f32),
-                jax.ShapeDtypeStruct(vector, f32),
+                jax.ShapeDtypeStruct((1, LANES), f32),
                 jax.ShapeDtypeStruct((nmem, *vector), f32),
             ),
             in_specs=[pl.BlockSpec(memory_space=pltpu.MemorySpace.HBM)],
@@ -457,8 +467,8 @@
                 pltpu.VMEM((levels, 5, *vector), f32),
                 pltpu.VMEM((rows + 2 * REACH, 3, *vector), f32),
                 pltpu.VMEM((nmem, *vector), f32),
-                pltpu.VMEM((nmem, *vector), f32),
-                pltpu.VMEM((nsx * nsy, *vector), f32),
+                pltpu.VMEM((nmem, 1, LANES), f32),
+                pltpu.VMEM((nsx * nsy, 1, LANES), f32),
                 dma((2,)),
                 dma((4,)),
                 dma((2,)),
@@ -470,6 +480,7 @@
                 dma((1,)),
                 dma((2,)),
                 dma((2,)),
+                pltpu.SemaphoreType.REGULAR((2,)),
             ],
             compiler_params=pltpu.CompilerParams(collective_id=0, has_side_effects=True, vmem_limit_bytes=VMEM_GRANT),
             name="gather",

time: 24.2 us -> 23.6 us (0.975)
  the two profiles are of different devices: /device:TPU:0 before, /device:TPU:1 now
where the time goes in v4:
time: 23.6 us; the launch traced here: 23.5 us
  Pallas kernels  22.9 us (97%)
  between operations  0.64 us (3%)
    pallas_call x1, Pallas kernels, local(): pl.pallas_call(functools.partial(gather, nmem, nsx, nsy), out_shape=(jax....  22.1 us
    pallas_call x1, Pallas kernels, local(): pl.pallas_call(functools.partial(scale, count), out_shape=(jax.ShapeDtype...  0.79 us

profile of v4, /device:TPU:1, one launch (start us, length us, event | category | flops | bytes accessed | tf_op | source)
XLA Modules:
  0.0 23.5 jit_solution(3209499574315759791)
XLA Ops:
  0.6 22.1 %gather.1 = (f32[2,128,128]{2,1,0:T(8,128)S(1)}, f32[1,128]{1,0:T(1,128)S(1)}, f32[8,8,128]{2,1,0:T(8,128)S(1)}) custom-call(bf16[4,8,48,768]{3,2,1,0:T(8,128)(2,1)} %child_ref.1), custom_call_target="tpu_custom_call" | custom-call | tf_op jit(solution)/shard_map/gather/pallas_call | solution.py:442
  22.7 0.8 %scale.1 = (f32[1,16,256]{2,1,0:T(8,128)}, f32[8,16,256]{2,1,0:T(8,128)}) custom-call(f32[2,128,128]{2,1,0:T(8,128)S(1)} %get-tuple-element.5.z_ref, f32[1,128]{1,0:T(1,128)S(1)} %get-tuple-element.6.all_ref, f32[8,8,128]{2,1,0:T(8,128)S(1)} %get-tuple-element.7.means_ref), custom_call_target="tpu_custom_call" | custom-call | tf_op jit(solution)/shard_map/scale/pallas_call | solution.py:489

commit v5 on v4

--- a/solution.py
+++ b/solution.py
@@ -135,13 +135,19 @@
     def greet(sem, friend):
         pl.semaphore_signal(sem, inc=1, device_id=friend, device_id_type=MESH)
 
-    def greet_around(sem):
+    fellows = (mem, peers[0])
+
+    def greet_around(sem, whom):
         for a in (-1, 0, 1):
             for b in (-1, 0, 1):
                 if (a, b) != (0, 0):
                     inside = (sx + a >= 0) & (sx + a < nsx) & (sy + b >= 0) & (sy + b < nsy)
-                    friend = at(x=lax.rem(sx + a + nsx, nsx), y=lax.rem(sy + b + nsy, nsy))
-                    pl.when(inside)(lambda: greet(sem, friend))
+                    x, y2 = lax.rem(sx + a + nsx, nsx), lax.rem(sy + b + nsy, nsy)
+
+                    @pl.when(inside)
+                    def _():
+                        for m in whom:
+                            greet(sem, at(m=m, x=x, y=y2))
 
     tiles_x = 3 - jnp.where(sx == 0, 1, 0) - jnp.where(sx == nsx - 1, 1, 0)
     tiles_y = 3 - jnp.where(sy == 0, 1, 0) - jnp.where(sy == nsy - 1, 1, 0)
@@ -149,7 +155,7 @@
     barrier = pltpu.get_barrier_semaphore()
     for p in peers:
         greet(barrier, at(m=p))
-    greet_around(barrier)
+    greet_around(barrier, fellows)
 
     zero = jnp.zeros((SUB, LANES), jnp.float32)
 
@@ -195,6 +201,11 @@
                 for j, value in enumerate((up - down, left + right, left - right)):
                     psend[half, owner, 4 + 6 * i2 + 2 * j + c] = value
                     within += value * value
+    pl.semaphore_wait(barrier, len(peers) + 2 * around)
+    greet_around(known.at[0], (mem,))
+    for n in (3, 1, 2, 4, 0, 5, 6):
+        post(0, 4, n, 1)
+
     def clear_rows(first):
         for row in range(first, first + REACH):
             for v in range(3):
@@ -226,11 +237,6 @@
                 packed = jnp.where(mine, both, packed)
         pack[d] = packed
 
-    pl.semaphore_wait(barrier, len(peers) + around)
-    greet_around(known.at[0])
-    for n in (3, 1, 2, 4, 0, 5, 6):
-        post(0, 4, n, 1)
-
     @pl.when(sy < nsy - 1)
     def _():
         send(pack, from_left, (e_send.at[0], e_recv.at[0]), at(y=lax.rem(sy + 1, nsy)))
@@ -260,7 +266,7 @@
     hbuf[0] = hsend[ring + y]
 
     pl.semaphore_wait(known.at[0], around)
-    greet_around(known.at[1])
+    greet_around(known.at[1], (mem,))
 
     settle(rbuf.at[pl.ds(1, nmem - 1), pl.ds(0, 4)], p1_sem.at[1], True)
     var = within
@@ -275,7 +281,7 @@
             abuf[v, o] = anom
             var += anom * anom
     s1[0] = jnp.sum(var, axis=0, keepdims=True)
-    for n, p in enumerate(peers):
+    for n, p in enumerate(peers[ring:]):
         send(s1.at[0], s1.at[n + 1], (s1_sem.at[0], s1_sem.at[1]), at(m=p))
     for n in range(nmem - 1):
         post(10, 6, n, 3)
@@ -347,11 +353,12 @@
     for v in range(3):
         q[REACH + edge_row, v] = msg[mem, v]
 
-    settle(s1.at[pl.ds(1, nmem - 1)], s1_sem.at[1], True)
+    settle(s1.at[pl.ds(1, ring - 1)], s1_sem.at[1], True)
     pl.semaphore_wait(known.at[1], around)
     s2[0] = jnp.sum(s1[...], axis=0)
-    for n, (a, b) in enumerate(plane_peers):
-        send(s2.at[0], s2.at[n + 1], (s2_sem.at[0], s2_sem.at[1]), at(x=a, y=b))
+    others = [(m, a, b) for a, b in plane_peers for m in fellows] + [(peers[0], sx, sy)]
+    for n, (m, a, b) in enumerate(others):
+        send(s2.at[0], s2.at[n + 1], (s2_sem.at[0], s2_sem.at[1]), at(m, a, b))
 
     settle(rbuf.at[pl.ds(1, nmem - 1), pl.ds(10, 6)], p1_sem.at[3], True)
     cells_of_row(1, 3)
@@ -399,18 +406,18 @@
         for c in range(2):
             z_ref[c, pl.ds(i, levels, stride=rows), :] = out[:, c * LANES : (c + 1) * LANES]
 
-    settle(s2.at[pl.ds(1, len(plane))], s2_sem.at[1], True)
+    settle(s2.at[pl.ds(1, len(others))], s2_sem.at[1], True)
     all_ref[...] = jnp.sum(s2[...], axis=0)
 
     settle(rbuf.at[pl.ds(1, nmem - 1)], p1_sem.at[0], False)
     pl.when(sy < nsy - 1)(lambda: settle(pack, e_send.at[0], False))
     pl.when(sy > 0)(lambda: settle(pack, e_send.at[1], False))
     settle(hsend.at[pl.ds(0, nmem - 1)], h_sem.at[0], False)
-    settle(s1.at[pl.ds(0, nmem - 1)], s1_sem.at[0], False)
+    settle(s1.at[pl.ds(1, ring - 1)], s1_sem.at[0], False)
     settle(mmsg.at[pl.ds(0, nmem - 1)], m_sem.at[0], False)
     settle(msg.at[pl.ds(0, nmem - 1)], q_sem.at[0], False)
     pl.when(sends_down | sends_up)(lambda: settle(q.at[pl.ds(0, levels)], n_send.at[0], False))
-    settle(s2.at[pl.ds(0, len(plane))], s2_sem.at[0], False)
+    settle(s2.at[pl.ds(1, len(others))], s2_sem.at[0], False)
 
 
 def scale(count, z_ref, all_ref, means_ref, mean_ref, cov_ref):
@@ -467,8 +474,8 @@
                 pltpu.VMEM((levels, 5, *vector), f32),
                 pltpu.VMEM((rows + 2 * REACH, 3, *vector), f32),
                 pltpu.VMEM((nmem, *vector), f32),
-                pltpu.VMEM((nmem, 1, LANES), f32),
-                pltpu.VMEM((nsx * nsy, 1, LANES), f32),
+                pltpu.VMEM((nmem // 2, 1, LANES), f32),
+                pltpu.VMEM((2 * nsx * nsy, 1, LANES), f32),
                 dma((2,)),
                 dma((4,)),
                 dma((2,)),

time: 23.6 us -> 23 us (0.975)
  Pallas kernels: 22.9 us -> 22.2 us
    pallas_call x1, Pallas kernels: 22.1 us -> 21.4 us  [local(): pl.pallas_call(functools.partial(gather, nmem, nsx, nsy), out_shape=(jax....]
where the time goes in v5:
time: 23 us; the launch traced here: 22.9 us
  Pallas kernels  22.2 us (97%)
  between operations  0.64 us (3%)
    pallas_call x1, Pallas kernels, local(): pl.pallas_call(functools.partial(gather, nmem, nsx, nsy), out_shape=(jax....  21.4 us
    pallas_call x1, Pallas kernels, local(): pl.pallas_call(functools.partial(scale, count), out_shape=(jax.ShapeDtype...  0.79 us

profile of v5, /device:TPU:1, one launch (start us, length us, event | category | flops | bytes accessed | tf_op | source)
XLA Modules:
  0.0 22.9 jit_solution(14020824288003393167)
XLA Ops:
  0.6 21.4 %gather.1 = (f32[2,128,128]{2,1,0:T(8,128)S(1)}, f32[1,128]{1,0:T(1,128)S(1)}, f32[8,8,128]{2,1,0:T(8,128)S(1)}) custom-call(bf16[4,8,48,768]{3,2,1,0:T(8,128)(2,1)} %child_ref.1), custom_call_target="tpu_custom_call" | custom-call | tf_op jit(solution)/shard_map/gather/pallas_call | solution.py:449
  22.1 0.8 %scale.1 = (f32[1,16,256]{2,1,0:T(8,128)}, f32[8,16,256]{2,1,0:T(8,128)}) custom-call(f32[2,128,128]{2,1,0:T(8,128)S(1)} %get-tuple-element.5.z_ref, f32[1,128]{1,0:T(1,128)S(1)} %get-tuple-element.6.all_ref, f32[8,8,128]{2,1,0:T(8,128)S(1)} %get-tuple-element.7.means_ref), custom_call_target="tpu_custom_call" | custom-call | tf_op jit(solution)/shard_map/scale/pallas_call | solution.py:496

commit v6 on v5

--- a/solution.py
+++ b/solution.py
@@ -245,28 +245,32 @@
     def _():
         send(pack, from_right, (e_send.at[1], e_recv.at[1]), at(y=lax.rem(sy + nsy - 1, nsy)))
 
-    for n in range(nmem - 1):
-        post(4, 6, n, 2)
-    for n in range(0):
-        post(10, 6, n, 3)
+    late = sy + 2 * (sx // 2) >= 4
+
+    def post_edge_rows(some):
+        for n in some:
+            post(4, 6, n, 2)
+
+    pl.when(~late)(lambda: post_edge_rows(range(nmem - 1)))
     for k in range(16):
         rbuf[0, k] = psend[1, y, k]
+
+    pl.semaphore_wait(known.at[0], around)
+    greet_around(known.at[1], (mem,))
+    pl.when(late)(lambda: post_edge_rows(range(7)))
 
     pl.when(sy > 0)(lambda: settle(from_left, e_recv.at[0], True))
     pl.when(sy < nsy - 1)(lambda: settle(from_right, e_recv.at[1], True))
     for d in range(nmem):
         hsend[d] = jnp.where((lane & 4) == 0, from_right[d], from_left[d])
-    for n, (p, spot) in enumerate(zip(peers, spots)):
-        send(
-            hsend.at[(1 - steps[n][0]) * ring + spot],
-            hbuf.at[n + 1],
-            (h_sem.at[0], h_sem.at[1]),
-            at(m=p),
-        )
+
+    def pass_edges():
+        for n, (p, spot) in enumerate(zip(peers, spots)):
+            owner = (1 - steps[n][0]) * ring + spot
+            send(hsend.at[owner], hbuf.at[n + 1], (h_sem.at[0], h_sem.at[1]), at(m=p))
+
+    pl.when(~late)(pass_edges)
     hbuf[0] = hsend[ring + y]
-
-    pl.semaphore_wait(known.at[0], around)
-    greet_around(known.at[1], (mem,))
 
     settle(rbuf.at[pl.ds(1, nmem - 1), pl.ds(0, 4)], p1_sem.at[1], True)
     var = within
@@ -283,6 +287,7 @@
     s1[0] = jnp.sum(var, axis=0, keepdims=True)
     for n, p in enumerate(peers[ring:]):
         send(s1.at[0], s1.at[n + 1], (s1_sem.at[0], s1_sem.at[1]), at(m=p))
+    pl.when(late)(pass_edges)
     for n in range(nmem - 1):
         post(10, 6, n, 3)
     for l in range(levels):
@@ -315,6 +320,16 @@
 
         lax.fori_loop(0, 2, column, 0)
 
+    others = [(m, a, b) for a, b in plane_peers for m in fellows] + [(peers[0], sx, sy)]
+
+    def spread_on():
+        settle(s1.at[pl.ds(1, ring - 1)], s1_sem.at[1], True)
+        pl.semaphore_wait(known.at[1], around)
+        s2[0] = jnp.sum(s1[...], axis=0)
+        for n, (m, a, b) in enumerate(others):
+            send(s2.at[0], s2.at[n + 1], (s2_sem.at[0], s2_sem.at[1]), at(m, a, b))
+
+    pl.when(late)(spread_on)
     settle(rbuf.at[pl.ds(1, nmem - 1), pl.ds(4, 6)], p1_sem.at[2], True)
     cells_of_row(0, 0)
     settle(hbuf.at[pl.ds(1, nmem - 1)], h_sem.at[1], True)
@@ -353,12 +368,7 @@
     for v in range(3):
         q[REACH + edge_row, v] = msg[mem, v]
 
-    settle(s1.at[pl.ds(1, ring - 1)], s1_sem.at[1], True)
-    pl.semaphore_wait(known.at[1], around)
-    s2[0] = jnp.sum(s1[...], axis=0)
-    others = [(m, a, b) for a, b in plane_peers for m in fellows] + [(peers[0], sx, sy)]
-    for n, (m, a, b) in enumerate(others):
-        send(s2.at[0], s2.at[n + 1], (s2_sem.at[0], s2_sem.at[1]), at(m, a, b))
+    pl.when(~late)(spread_on)
 
     settle(rbuf.at[pl.ds(1, nmem - 1), pl.ds(10, 6)], p1_sem.at[3], True)
     cells_of_row(1, 3)

time: 23 us -> 22.8 us (level)
  no operation moved by 1% of the time
where the time goes in v6:
time: 22.8 us; the launch traced here: 22.7 us
  Pallas kernels  22 us (96%)
  between operations  0.64 us (3%)
    pallas_call x1, Pallas kernels, local(): pl.pallas_call(functools.partial(gather, nmem, nsx, nsy), out_shape=(jax....  21.2 us
    pallas_call x1, Pallas kernels, local(): pl.pallas_call(functools.partial(scale, count), out_shape=(jax.ShapeDtype...  0.79 us

profile of v6, /device:TPU:1, one launch (start us, length us, event | category | flops | bytes accessed | tf_op | source)
XLA Modules:
  0.0 22.7 jit_solution(9280664119608284594)
XLA Ops:
  0.6 21.2 %gather.1 = (f32[2,128,128]{2,1,0:T(8,128)S(1)}, f32[1,128]{1,0:T(1,128)S(1)}, f32[8,8,128]{2,1,0:T(8,128)S(1)}) custom-call(bf16[4,8,48,768]{3,2,1,0:T(8,128)(2,1)} %child_ref.1), custom_call_target="tpu_custom_call" | custom-call | tf_op jit(solution)/shard_map/gather/pallas_call | solution.py:459
  21.9 0.8 %scale.1 = (f32[1,16,256]{2,1,0:T(8,128)}, f32[8,16,256]{2,1,0:T(8,128)}) custom-call(f32[2,128,128]{2,1,0:T(8,128)S(1)} %get-tuple-element.5.z_ref, f32[1,128]{1,0:T(1,128)S(1)} %get-tuple-element.6.all_ref, f32[8,8,128]{2,1,0:T(8,128)S(1)} %get-tuple-element.7.means_ref), custom_call_target="tpu_custom_call" | custom-call | tf_op jit(solution)/shard_map/scale/pallas_call | solution.py:506

commit v7 on v6

--- a/solution.py
+++ b/solution.py
@@ -288,8 +288,11 @@
     for n, p in enumerate(peers[ring:]):
         send(s1.at[0], s1.at[n + 1], (s1_sem.at[0], s1_sem.at[1]), at(m=p))
     pl.when(late)(pass_edges)
-    for n in range(nmem - 1):
-        post(10, 6, n, 3)
+    def post_inner_rows():
+        for n in range(nmem - 1):
+            post(10, 6, n, 3)
+
+    pl.when(~late)(post_inner_rows)
     for l in range(levels):
         mmsg[l] = zero
         for v in range(4):
@@ -329,8 +332,16 @@
         for n, (m, a, b) in enumerate(others):
             send(s2.at[0], s2.at[n + 1], (s2_sem.at[0], s2_sem.at[1]), at(m, a, b))
 
-    pl.when(late)(spread_on)
-    settle(rbuf.at[pl.ds(1, nmem - 1), pl.ds(4, 6)], p1_sem.at[2], True)
+    def edge_rows_arrived():
+        settle(rbuf.at[pl.ds(1, nmem - 1), pl.ds(4, 6)], p1_sem.at[2], True)
+
+    @pl.when(late)
+    def _():
+        edge_rows_arrived()
+        post_inner_rows()
+        spread_on()
+
+    pl.when(~late)(edge_rows_arrived)
     cells_of_row(0, 0)
     settle(hbuf.at[pl.ds(1, nmem - 1)], h_sem.at[1], True)
     total = hbuf[0]

time: 22.8 us -> 22.8 us (level)
  no operation moved by 1% of the time
where the time goes in v7:
time: 22.8 us; the launch traced here: 22.7 us
  Pallas kernels  22 us (96%)
  between operations  0.64 us (3%)
    pallas_call x1, Pallas kernels, local(): pl.pallas_call(functools.partial(gather, nmem, nsx, nsy), out_shape=(jax....  21.2 us
    pallas_call x1, Pallas kernels, local(): pl.pallas_call(functools.partial(scale, count), out_shape=(jax.ShapeDtype...  0.79 us

profile of v7, /device:TPU:1, one launch (start us, length us, event | category | flops | bytes accessed | tf_op | source)
XLA Modules:
  0.0 22.7 jit_solution(13326601176334879997)
XLA Ops:
  0.6 21.2 %gather.1 = (f32[2,128,128]{2,1,0:T(8,128)S(1)}, f32[1,128]{1,0:T(1,128)S(1)}, f32[8,8,128]{2,1,0:T(8,128)S(1)}) custom-call(bf16[4,8,48,768]{3,2,1,0:T(8,128)(2,1)} %child_ref.1), custom_call_target="tpu_custom_call" | custom-call | tf_op jit(solution)/shard_map/gather/pallas_call | solution.py:470
  21.9 0.8 %scale.1 = (f32[1,16,256]{2,1,0:T(8,128)}, f32[8,16,256]{2,1,0:T(8,128)}) custom-call(f32[2,128,128]{2,1,0:T(8,128)S(1)} %get-tuple-element.5.z_ref, f32[1,128]{1,0:T(1,128)S(1)} %get-tuple-element.6.all_ref, f32[8,8,128]{2,1,0:T(8,128)S(1)} %get-tuple-element.7.means_ref), custom_call_target="tpu_custom_call" | custom-call | tf_op jit(solution)/shard_map/scale/pallas_call | solution.py:517

commit v8 on v7

--- a/solution.py
+++ b/solution.py
@@ -91,15 +91,6 @@
             "sy": sy if y is None else y,
         }
 
-    loads = []
-    for half, owner_z in enumerate((1 - z, z)):
-        first = pl.multiple_of(owner_z * half_rows, SUB)
-        copy = pltpu.make_async_copy(
-            child_ref.at[:, :, pl.ds(first, half_rows), :], xbuf.at[half], ld_sem.at[half]
-        )
-        copy.start()
-        loads.append(copy)
-
     steps = [(1, 0), (1, 1), (1, 3), (1, 2), (0, 2), (0, 1), (0, 3)]
     spots = [lax.rem(y + b, ring) for _, b in steps]
     peers = [lax.rem(z + a, 2) * ring + spot for (a, _), spot in zip(steps, spots)]
@@ -155,6 +146,16 @@
     barrier = pltpu.get_barrier_semaphore()
     for p in peers:
         greet(barrier, at(m=p))
+
+    loads = []
+    for half, owner_z in enumerate((1 - z, z)):
+        first = pl.multiple_of(owner_z * half_rows, SUB)
+        copy = pltpu.make_async_copy(
+            child_ref.at[:, :, pl.ds(first, half_rows), :], xbuf.at[half], ld_sem.at[half]
+        )
+        copy.start()
+        loads.append(copy)
+
     greet_around(barrier, fellows)
 
     zero = jnp.zeros((SUB, LANES), jnp.float32)

time: 22.8 us -> 22.9 us (level)
  no operation moved by 1% of the time
where the time goes in v8:
time: 22.9 us; the launch traced here: 22.8 us
  Pallas kernels  22.1 us (97%)
  between operations  0.64 us (3%)
    pallas_call x1, Pallas kernels, local(): pl.pallas_call(functools.partial(gather, nmem, nsx, nsy), out_shape=(jax....  21.3 us
    pallas_call x1, Pallas kernels, local(): pl.pallas_call(functools.partial(scale, count), out_shape=(jax.ShapeDtype...  0.79 us

profile of v8, /device:TPU:1, one launch (start us, length us, event | category | flops | bytes accessed | tf_op | source)
XLA Modules:
  0.0 22.8 jit_solution(6309368026958501838)
XLA Ops:
  0.6 21.3 %gather.1 = (f32[2,128,128]{2,1,0:T(8,128)S(1)}, f32[1,128]{1,0:T(1,128)S(1)}, f32[8,8,128]{2,1,0:T(8,128)S(1)}) custom-call(bf16[4,8,48,768]{3,2,1,0:T(8,128)(2,1)} %child_ref.1), custom_call_target="tpu_custom_call" | custom-call | tf_op jit(solution)/shard_map/gather/pallas_call | solution.py:471
  22.0 0.8 %scale.1 = (f32[1,16,256]{2,1,0:T(8,128)}, f32[8,16,256]{2,1,0:T(8,128)}) custom-call(f32[2,128,128]{2,1,0:T(8,128)S(1)} %get-tuple-element.5.z_ref, f32[1,128]{1,0:T(1,128)S(1)} %get-tuple-element.6.all_ref, f32[8,8,128]{2,1,0:T(8,128)S(1)} %get-tuple-element.7.means_ref), custom_call_target="tpu_custom_call" | custom-call | tf_op jit(solution)/shard_map/scale/pallas_call | solution.py:518
